TPU v7x, 32 devices: a whole 2x2x4 slice. The times are simulated.
32 devices in a mesh: gx: 4 (over x, core), gy: 2 (over y), gz: 4 (over z).
Axes of the slice: x: 2, y: 2, z: 4, core: 2. Of those that a mesh axis runs over, the one named last changes fastest.
Arguments:
- offsets: float32 [3, 4, 4, 8, 128], P(None, 'gx', 'gy', 'gz'), may hold values from 0 to 11, as said below
- type_ids: int32 [4, 4, 8, 128], P('gx', 'gy', 'gz'), may hold values from 0 to 1
- neighbours: int32 [4, 4, 8, 27], P('gx', 'gy', 'gz'), may hold values from 0 to 48, as said below
- type_chi: float32 [2], replicated, may hold values from 3 to 7
- type_eta: float32 [2], replicated, may hold values from 6 to 12
- type_gamma: float32 [2], replicated, may hold values from 0.5 to 1
Outputs:
- charges: float32 [4, 4, 8, 128], P('gx', 'gy', 'gz')
- residuals: float32 [2, 4, 4, 8, 128], P(None, 'gx', 'gy', 'gz')
Inputs may be any that keep to these rules, and one draw needn't show every extreme that they name: `neighbours`: each tile's row lists the tile itself and some of the 26 cells around it, each at most once, as indices into its device's block padded by one cell on every side (3) x (4) x (4) in first-dimension-major order; unused slots hold (3) * 4 * 4. Two tiles list each other with opposite displacements or not at all. `offsets`: any two atoms of the box lie at least 0.8 A apart.
All inputs are finite; a program needn't handle non-finite values.
Results may differ from a plain program's by a relative error of at most 0.0003.
Values sent between devices are 32-bit elements; how exact they have to be, the bound alone decides.
A program may use at most 64 MiB of HBM per device.

v0:
```python
import itertools

import jax
import jax.numpy as jnp
from jax import lax
from jax.experimental import pallas as pl
from jax.experimental.pallas import tpu as pltpu
from jax.sharding import PartitionSpec as P

ITERS = 3
CELL_EDGE = 11.0
CUTOFF = 10.0
COULOMB = 14.4
AXES = ("gx", "gy", "gz")
FAR = 1000.0
MESH = pl.DeviceIdType.MESH
STEPS = [d for d in itertools.product((-1, 0, 1), repeat=3)]
REMOTE = [d for d in STEPS if d != (0, 0, 0)]


def rounded_sides(step, cells):
    source, target = [], []
    for d, c in zip(step, cells):
        if d == 0:
            source.append(pl.ds(1, c))
            target.append(pl.ds(1, c))
        elif d > 0:
            source.append(pl.ds(c, 1))
            target.append(pl.ds(0, 1))
        else:
            source.append(pl.ds(1, 1))
            target.append(pl.ds(c + 1, 1))
    return tuple(source), tuple(target)


def make_kernel(sizes, groups, cells, atoms, types, rows):
    width = tuple(c + 2 for c in cells)
    tiles = cells[0] * cells[1] * cells[2]
    local = list(itertools.product(*[range(c) for c in cells]))
    padded = list(itertools.product(*[range(w) for w in width]))
    own = tuple(slice(1, 1 + c) for c in cells)
    group_sizes = []
    for axes in groups:
        count = 1
        for a in axes:
            count = count * sizes[a]
        group_sizes.append(count)

    def linear(place):
        return (place[0] * width[1] + place[1]) * width[2] + place[2]

    def kernel(*refs):
        off_ref, type_ref, list_ref, chi_ref, eta_ref, gamma_ref, charge_ref, resid_ref = refs[:8]
        (fields, geometry, columns, far, blocks, sums, resid, along, *rest) = refs[8:]
        images = rest[:ITERS]
        rest = rest[ITERS:]
        parts = rest[: len(groups)]
        halo_send, halo_recv, sum_send, sum_recv = rest[len(groups) :]

        me = {a: lax.axis_index(a) for a in AXES}

        def neighbour(step):
            return tuple(
                lax.rem(me[a] + (d + sizes[a]), sizes[a]) for a, d in zip(AXES, step)
            )

        def member(axes, hop):
            rank = 0
            count = 1
            for a in axes:
                rank = rank * sizes[a] + me[a]
                count = count * sizes[a]
            rank = lax.rem(rank + hop, count)
            place = dict(me)
            for a in reversed(axes):
                place[a] = lax.rem(rank, sizes[a])
                rank = rank // sizes[a]
            return tuple(place[a] for a in AXES)

        def lookup(kinds, table):
            result = jnp.zeros(kinds.shape, jnp.float32)
            for k in range(types):
                result = jnp.where(kinds == float(k), table[k], result)
            return result

        for x, y, z in local:
            for f in range(3):
                fields[x + 1, y + 1, z + 1, f : f + 1, :] = off_ref[f, x, y, z : z + 1, :]
            fields[x + 1, y + 1, z + 1, 3:4, :] = type_ref[x, y, z : z + 1, :].astype(jnp.float32)

        barrier = pltpu.get_barrier_semaphore()
        greeted = 0
        for axes, count in zip(groups, group_sizes):
            for hop in range(1, count):
                pl.semaphore_signal(
                    barrier, inc=1, device_id=member(axes, hop), device_id_type=MESH
                )
                greeted += 1
        if len(groups) > 1:
            for step in REMOTE:
                pl.semaphore_signal(
                    barrier, inc=1, device_id=neighbour(step), device_id_type=MESH
                )
                greeted += 1
        pl.semaphore_wait(barrier, greeted)

        def halo(buffer, stage):
            copies = []
            for n, step in enumerate(REMOTE):
                source, target = rounded_sides(step, cells)
                copies.append(
                    pltpu.make_async_remote_copy(
                        src_ref=buffer.at[source],
                        dst_ref=buffer.at[target],
                        send_sem=halo_send.at[n],
                        recv_sem=halo_recv.at[stage, n],
                        device_id=neighbour(step),
                        device_id_type=MESH,
                    )
                )
            for copy in copies:
                copy.start()
            return copies

        def finish(copies):
            for copy in copies:
                copy.wait_recv()
            for copy in copies:
                copy.wait_send()

        moving = halo(fields, 0)

        def tenth(values, f, place):
            return (values + CELL_EDGE * (place[f] - 1.0)) * (1.0 / CUTOFF)

        def sigma(kinds):
            root = lax.rsqrt(lookup(kinds, gamma_ref))
            return root * root * root * (CUTOFF**-1.5)

        for t, (x, y, z) in enumerate(local):
            place = (x + 1, y + 1, z + 1)
            for f in range(4):
                row = fields[x + 1, y + 1, z + 1, f : f + 1, :]
                row = tenth(row, f, place) if f < 3 else sigma(row)
                columns[t, f] = jnp.transpose(jnp.broadcast_to(row, (atoms, atoms)))
        entries = jnp.concatenate(
            [list_ref[x, y, z : z + 1, :] - linear((x + 1, y + 1, z + 1)) for x, y, z in local], 0
        )
        for n, step in enumerate(STEPS):
            found = jnp.max(
                jnp.where(entries == linear(step), 1.0, 0.0), axis=1, keepdims=True
            )
            far[n] = jnp.broadcast_to((1.0 - found) * FAR, (tiles, atoms))

        finish(moving)

        for x, y, z in padded:
            place = (x, y, z)
            kinds = fields[x, y, z, 3:4, :]
            for f in range(3):
                geometry[x, y, z, f : f + 1, :] = tenth(fields[x, y, z, f : f + 1, :], f, place)
            geometry[x, y, z, 3:4, :] = sigma(kinds)
            resid[x, y, z, 0:1, :] = -lookup(kinds, chi_ref)
            resid[x, y, z, 1:2, :] = jnp.full((1, atoms), -1.0, jnp.float32)

        slabs = atoms // rows

        def spot(index):
            t = index // slabs
            at = pl.multiple_of((index % slabs) * rows, rows)
            z = t % cells[2]
            y = (t // cells[2]) % cells[1]
            x = t // (cells[2] * cells[1])
            return t, at, (x + 1, y + 1, z + 1)

        def build(index, carry):
            t, at, (x, y, z) = spot(index)
            own_part = [columns[t, f, pl.ds(at, rows), :] for f in range(4)]
            total_s = jnp.zeros((rows, atoms), jnp.float32)
            total_t = jnp.zeros((rows, atoms), jnp.float32)
            for n, (a, b, c) in enumerate(STEPS):
                near = [geometry[x + a, y + b, z + c, f : f + 1, :] for f in range(4)]
                near[0] = near[0] + far[n, pl.ds(t, 1), :]
                dx = near[0] - own_part[0]
                dy = near[1] - own_part[1]
                dz = near[2] - own_part[2]
                square = dx * dx + dy * dy + dz * dz
                if (a, b, c) == (0, 0, 0):
                    i = lax.broadcasted_iota(jnp.int32, (rows, atoms), 0) + at
                    j = lax.broadcasted_iota(jnp.int32, (rows, atoms), 1)
                    square = jnp.where(i == j, 4.0, square)
                u = square * lax.rsqrt(square)
                w = jnp.maximum(1.0 - u, 0.0)
                w = w * w
                w = w * w
                shape = (u + 0.5) * (square + 0.2) - 0.05
                cube = square * u + own_part[3] * near[3]
                block = w * shape * jnp.exp2(jnp.log2(cube) * (-1.0 / 3.0))
                blocks[t, n, pl.ds(at, rows), :] = block
                total_s = total_s + block * resid[x + a, y + b, z + c, 0:1, :]
                total_t = total_t - block
            sums[t, 0, pl.ds(at, rows), :] = total_s
            sums[t, 1, pl.ds(at, rows), :] = total_t
            return carry

        def again(index, carry):
            t, at, (x, y, z) = spot(index)
            total_s = jnp.zeros((rows, atoms), jnp.float32)
            total_t = jnp.zeros((rows, atoms), jnp.float32)
            for n, (a, b, c) in enumerate(STEPS):
                block = blocks[t, n, pl.ds(at, rows), :]
                total_s = total_s + block * resid[x + a, y + b, z + c, 0:1, :]
                total_t = total_t + block * resid[x + a, y + b, z + c, 1:2, :]
            sums[t, 0, pl.ds(at, rows), :] = total_s
            sums[t, 1, pl.ds(at, rows), :] = total_t
            return carry

        scale = 20.0 * COULOMB / CUTOFF
        ones = jnp.ones((8, atoms), jnp.float32)
        eta = [lookup(fields[x + 1, y + 1, z + 1, 3:4, :], eta_ref) for x, y, z in local]

        def collect(image):
            for t, (x, y, z) in enumerate(local):
                for s in range(2):
                    row = lax.dot_general(
                        ones,
                        sums[t, s],
                        (((1,), (1,)), ((), ())),
                        precision=lax.Precision.HIGHEST,
                        preferred_element_type=jnp.float32,
                    )[0:1]
                    here = resid[x + 1, y + 1, z + 1, s : s + 1, :]
                    image[x + 1, y + 1, z + 1, s : s + 1, :] = eta[t] * here + scale * row

        lane = lax.broadcasted_iota(jnp.int32, (2, atoms), 1)

        def over_own(values):
            return jnp.sum(jnp.sum(values, axis=(0, 1, 2)), axis=1, keepdims=True)

        def packed(values):
            message = jnp.zeros((2, atoms), jnp.float32)
            for k, value in enumerate(values):
                message = jnp.where(lane == k, value, message)
            return message

        def start_sum(g, stage):
            axes, count = groups[g], group_sizes[g]
            start = sum(group_sizes[:g]) - g
            copies = []
            for hop in range(1, count):
                copies.append(
                    pltpu.make_async_remote_copy(
                        src_ref=parts[g].at[stage, 0],
                        dst_ref=parts[g].at[stage, hop],
                        send_sem=sum_send.at[start + hop - 1],
                        recv_sem=sum_recv.at[stage, start + hop - 1],
                        device_id=member(axes, hop),
                        device_id_type=MESH,
                    )
                )
            for copy in copies:
                copy.start()
            return copies

        def exchange(values, image, stage):
            parts[0][stage, 0] = packed(values)
            moving = halo(image, stage + 1) if stage + 1 < ITERS else []
            copies = start_sum(0, stage)
            for g in range(len(groups)):
                finish(copies)
                total = jnp.sum(parts[g][stage], axis=0)
                if g + 1 < len(groups):
                    parts[g + 1][stage, 0] = total
                    copies = start_sum(g + 1, stage)
            finish(moving)
            return [
                jnp.sum(jnp.where(lane == k, total, 0.0), axis=1, keepdims=True)
                for k in range(len(values))
            ]

        lax.fori_loop(0, tiles * slabs, build, 0)
        collect(images[0])
        direction = resid[own]
        norm_now, curvature = exchange(
            [over_own(direction * direction), over_own(direction * images[0][own])], images[0], 0
        )
        step_size = norm_now / curvature
        answer = jnp.zeros_like(direction)
        sum_answer = jnp.zeros_like(norm_now)
        along[...] = images[0][...]
        carried = (norm_now, norm_now, norm_now, jnp.zeros_like(norm_now))
        for iteration in range(ITERS):
            answer = answer + step_size * direction
            if iteration + 1 == ITERS:
                last = resid[own] - step_size * along[own]
                break
            resid[...] = resid[...] - step_size * along[...]
            lax.fori_loop(0, tiles * slabs, again, 0)
            image = images[iteration + 1]
            collect(image)
            here = resid[own]
            values = [over_own(here * here), over_own(here * image[own])]
            ends = iteration + 2 == ITERS
            if ends:
                values = values + [over_own(answer), over_own(here), over_own(direction)]
            norm_next, curvature, *others = exchange(values, image, iteration + 1)
            growth = norm_next / norm_now
            step_size = norm_next / (curvature - growth * norm_next / step_size)
            direction = here + growth * direction
            if ends:
                along[own] = image[own] + growth * along[own]
                totals = others[0] + step_size * (others[1] + growth * others[2])
            else:
                along[...] = image[...] + growth * along[...]
            norm_now = norm_next

        level = totals[0:1] / totals[1:2]
        for t, (x, y, z) in enumerate(local):
            charge_ref[x, y, z : z + 1, :] = 1000.0 * (
                answer[x, y, z, 0:1] - level * answer[x, y, z, 1:2]
            )
            for s in range(2):
                resid_ref[s, x, y, z : z + 1, :] = last[x, y, z, s : s + 1]

    scratch = [
        pltpu.VMEM(width + (4, atoms), jnp.float32),
        pltpu.VMEM(width + (4, atoms), jnp.float32),
        pltpu.VMEM((tiles, 4, atoms, atoms), jnp.float32),
        pltpu.VMEM((len(STEPS), tiles, atoms), jnp.float32),
        pltpu.VMEM((tiles, len(STEPS), atoms, atoms), jnp.float32),
        pltpu.VMEM((tiles, 2, atoms, atoms), jnp.float32),
        pltpu.VMEM(width + (2, atoms), jnp.float32),
        pltpu.VMEM(width + (2, atoms), jnp.float32),
    ]
    scratch += [pltpu.VMEM(width + (2, atoms), jnp.float32) for _ in range(ITERS)]
    scratch += [pltpu.VMEM((ITERS, count, 2, atoms), jnp.float32) for count in group_sizes]
    hops = sum(group_sizes) - len(groups)
    scratch += [
        pltpu.SemaphoreType.DMA((len(REMOTE),)),
        pltpu.SemaphoreType.DMA((ITERS, len(REMOTE))),
        pltpu.SemaphoreType.DMA((hops,)),
        pltpu.SemaphoreType.DMA((ITERS, hops)),
    ]
    return kernel, scratch


def solution(mesh):
    sizes = {a: mesh.shape[a] for a in AXES}
    devices = sizes["gx"] * sizes["gy"] * sizes["gz"]
    groups = (AXES,) if devices <= 64 else tuple((a,) for a in AXES)

    def per_device(offsets, type_ids, neighbours, type_chi, type_eta, type_gamma):
        cells = offsets.shape[1:4]
        atoms = offsets.shape[4]
        types = type_chi.shape[0]
        kernel, scratch = make_kernel(sizes, groups, cells, atoms, types, 32)
        vmem = pl.BlockSpec(memory_space=pltpu.VMEM)
        smem = pl.BlockSpec(memory_space=pltpu.SMEM)
        return pl.pallas_call(
            kernel,
            out_shape=(
                jax.ShapeDtypeStruct(cells + (atoms,), jnp.float32),
                jax.ShapeDtypeStruct((2,) + cells + (atoms,), jnp.float32),
            ),
            in_specs=[vmem, vmem, vmem, smem, smem, smem],
            out_specs=(vmem, vmem),
            scratch_shapes=scratch,
            compiler_params=pltpu.CompilerParams(
                collective_id=0, has_side_effects=True, vmem_limit_bytes=48 * 1024 * 1024
            ),
        )(offsets, type_ids, neighbours, type_chi, type_eta, type_gamma)

    placed = (
        P(None, "gx", "gy", "gz", None),
        P("gx", "gy", "gz", None),
        P("gx", "gy", "gz", None),
        P(),
        P(),
        P(),
    )
    return jax.shard_map(
        per_device,
        mesh=mesh,
        in_specs=placed,
        out_specs=(P("gx", "gy", "gz", None), P(None, "gx", "gy", "gz", None)),
        check_vma=False,
    )
```

profile of v0, /device:TPU:0, one launch (start us, length us, event | category | flops | bytes accessed | tf_op | source)
XLA Modules:
  0.0 49.2 jit_solution(9065795859513179252)
XLA Ops:
  0.6 0.0 copy-start
  0.6 0.7 %copy-done = f32[3,1,2,2,128]{4,3,2,1,0:T(2,128)S(1)} copy-done((f32[3,1,2,2,128]{4,3,2,1,0:T(2,128)S(1)}, f32[3,1,2,2,128]{4,3,2,1,0:T(2,128)}, u32[]{:S(2)}) %copy-start) | copy-done | bytes 6168
  1.3 0.0 copy-start.1
  1.3 0.7 %copy-done.1 = s32[1,2,2,128]{3,2,1,0:T(2,128)S(1)} copy-done((s32[1,2,2,128]{3,2,1,0:T(2,128)S(1)}, s32[1,2,2,128]{3,2,1,0:T(2,128)}, u32[]{:S(2)}) %copy-start.1) | copy-done | bytes 2072
  2.0 0.0 copy-start.2
  2.0 0.7 %copy-done.2 = s32[1,2,2,27]{3,2,1,0:T(2,128)S(1)} copy-done((s32[1,2,2,27]{3,2,1,0:T(2,128)S(1)}, s32[1,2,2,27]{3,2,1,0:T(2,128)}, u32[]{:S(2)}) %copy-start.2) | copy-done | bytes 456
  2.7 0.0 copy-start.3
  2.7 0.7 %copy-done.3 = f32[2]{0:T(128)S(1)} copy-done((f32[2]{0:T(128)S(1)}, f32[2]{0:T(128)}, u32[]{:S(2)}) %copy-start.3) | copy-done | bytes 32
  3.3 0.0 copy-start.4
  3.3 0.7 %copy-done.4 = f32[2]{0:T(128)S(1)} copy-done((f32[2]{0:T(128)S(1)}, f32[2]{0:T(128)}, u32[]{:S(2)}) %copy-start.4) | copy-done | bytes 32
  4.0 0.0 copy-start.5
  4.0 0.7 %copy-done.5 = f32[2]{0:T(128)S(1)} copy-done((f32[2]{0:T(128)S(1)}, f32[2]{0:T(128)}, u32[]{:S(2)}) %copy-start.5) | copy-done | bytes 32
  4.7 43.4 %shard_map.77 = (f32[1,2,2,128]{3,2,1,0:T(2,128)S(1)}, f32[2,1,2,2,128]{4,3,2,1,0:T(2,128)S(1)}) custom-call(f32[3,1,2,2,128]{4,3,2,1,0:T(2,128)S(1)} %copy-done, s32[1,2,2,128]{3,2,1,0:T(2,128)S(1)} %copy-done.1, s32[1,2,2,27]{3,2,1,0:T(2,128)S(1)} %copy-done.2, f32[2]{0:T(128)S(1)} %copy-done.3, f32[2]{0:T(128)S(1)} %copy-done.4, f32[2]{0:T(128)S(1)} %copy-done.5), custom_call_target="tpu_custom_call" | custom-call | tf_op jit(solution)/shard_map/pallas_call | solution.py:359
  48.0 0.6 %copy.10 = f32[1,2,2,128]{3,2,1,0:T(2,128)} copy(f32[1,2,2,128]{3,2,1,0:T(2,128)S(1)} %get-tuple-element.4) | data formatting | bytes 4096
  48.6 0.6 %copy.11 = f32[2,1,2,2,128]{4,3,2,1,0:T(2,128)} copy(f32[2,1,2,2,128]{4,3,2,1,0:T(2,128)S(1)} %get-tuple-element.5) | data formatting | bytes 8192
Async XLA Ops:
  0.6 0.7 %copy-start = (f32[3,1,2,2,128]{4,3,2,1,0:T(2,128)S(1)}, f32[3,1,2,2,128]{4,3,2,1,0:T(2,128)}, u32[]{:S(2)}) copy-start(f32[3,1,2,2,128]{4,3,2,1,0:T(2,128)} %refs_0_.1) | copy-start | bytes 18436
  1.3 0.7 %copy-start.1 = (s32[1,2,2,128]{3,2,1,0:T(2,128)S(1)}, s32[1,2,2,128]{3,2,1,0:T(2,128)}, u32[]{:S(2)}) copy-start(s32[1,2,2,128]{3,2,1,0:T(2,128)} %refs_1_.1) | copy-start | bytes 6148
  2.0 0.7 %copy-start.2 = (s32[1,2,2,27]{3,2,1,0:T(2,128)S(1)}, s32[1,2,2,27]{3,2,1,0:T(2,128)}, u32[]{:S(2)}) copy-start(s32[1,2,2,27]{3,2,1,0:T(2,128)} %refs_2_.1) | copy-start | bytes 1300
  2.7 0.7 %copy-start.3 = (f32[2]{0:T(128)S(1)}, f32[2]{0:T(128)}, u32[]{:S(2)}) copy-start(f32[2]{0:T(128)} %refs_3_.1) | copy-start | bytes 28
  3.3 0.7 %copy-start.4 = (f32[2]{0:T(128)S(1)}, f32[2]{0:T(128)}, u32[]{:S(2)}) copy-start(f32[2]{0:T(128)} %refs_4_.1) | copy-start | bytes 28
  4.0 0.7 %copy-start.5 = (f32[2]{0:T(128)S(1)}, f32[2]{0:T(128)}, u32[]{:S(2)}) copy-start(f32[2]{0:T(128)} %refs_5_.1) | copy-start | bytes 28
where the time goes:
time: 49.5 us; the launch traced here: 49.2 us
  Pallas kernels  43.4 us (88%)
  local copies, waits for them, and re-layouts  5.18 us (10%)
  between operations  0.65 us (1%)
    pallas_call x1, Pallas kernels, per_device(): pl.pallas_call(kernel, out_shape=(jax.ShapeDtypeStruct(cells + (atoms,),...  43.4 us
    unnamed x14, local copies, waits for them, and re-layouts  5.18 us

commit v1 on v0

v1 whole, which is shorter than its diff:
```python
import itertools

import jax
import jax.numpy as jnp
from jax import lax
from jax.experimental import pallas as pl
from jax.experimental.pallas import tpu as pltpu
from jax.sharding import PartitionSpec as P

ITERS = 3
CELL_EDGE = 11.0
CUTOFF = 10.0
COULOMB = 14.4
AXES = ("gx", "gy", "gz")
FAR = 1000.0
MESH = pl.DeviceIdType.MESH
STEPS = [d for d in itertools.product((-1, 0, 1), repeat=3)]
REMOTE = sorted((d for d in STEPS if d != (0, 0, 0)), key=lambda d: (-abs(d[2]), -abs(d[0])))
KINDS = 3


def kind_of(step):
    return 2 if step[2] else (1 if step[0] else 0)


def rounded_sides(step, cells):
    source, target = [], []
    for d, c in zip(step, cells):
        if d == 0:
            source.append(pl.ds(1, c))
            target.append(pl.ds(1, c))
        elif d > 0:
            source.append(pl.ds(c, 1))
            target.append(pl.ds(0, 1))
        else:
            source.append(pl.ds(1, 1))
            target.append(pl.ds(c + 1, 1))
    return tuple(source), tuple(target)


def make_kernel(sizes, groups, cells, atoms, types, rows):
    width = tuple(c + 2 for c in cells)
    tiles = cells[0] * cells[1] * cells[2]
    local = list(itertools.product(*[range(c) for c in cells]))
    padded = list(itertools.product(*[range(w) for w in width]))
    own = tuple(slice(1, 1 + c) for c in cells)
    group_sizes = []
    for axes in groups:
        count = 1
        for a in axes:
            count = count * sizes[a]
        group_sizes.append(count)
    boxes = (
        (pl.ds(0, cells[0]), pl.ds(0, 2), pl.ds(0, cells[2])),
        (pl.ds(0, 2), pl.ds(0, width[1]), pl.ds(0, cells[2])),
        (pl.ds(0, width[0]), pl.ds(0, width[1]), pl.ds(0, 2)),
    )

    def linear(place):
        return (place[0] * width[1] + place[1]) * width[2] + place[2]

    def reach(place):
        if not 1 <= place[2] <= cells[2]:
            return 2
        return 0 if all(1 <= p <= c for p, c in zip(place, cells)) else 1

    pairs = [[], [], []]
    for t, home in enumerate(local):
        split = [[], [], []]
        for n, step in enumerate(STEPS):
            place = tuple(h + 1 + d for h, d in zip(home, step))
            split[reach(place)].append((n, place))
        for kept, part in zip(pairs, split):
            kept.append((t, part))

    def kernel(*refs):
        hbm, (charge_ref, resid_ref) = refs[:6], refs[6:8]
        (off_ref, type_ref, list_ref, chi_ref, eta_ref, gamma_ref) = refs[8:14]
        (fields, geometry, columns, listed, blocks, sums, source, first, second, own_image) = refs[14:24]
        parts = refs[24 : 24 + len(groups)]
        load_sem, halo_send, halo_recv, sum_send, sum_recv = refs[24 + len(groups) :]

        loads = [
            pltpu.make_async_copy(a, b, load_sem.at[k])
            for k, (a, b) in enumerate(
                zip(hbm, (off_ref, type_ref, list_ref, chi_ref, eta_ref, gamma_ref))
            )
        ]
        for load in loads:
            load.start()

        me = {a: lax.axis_index(a) for a in AXES}

        def neighbour(step):
            return tuple(
                lax.rem(me[a] + (d + sizes[a]), sizes[a]) for a, d in zip(AXES, step)
            )

        def member(axes, hop):
            rank = 0
            count = 1
            for a in axes:
                rank = rank * sizes[a] + me[a]
                count = count * sizes[a]
            rank = lax.rem(rank + hop, count)
            place = dict(me)
            for a in reversed(axes):
                place[a] = lax.rem(rank, sizes[a])
                rank = rank // sizes[a]
            return tuple(place[a] for a in AXES)

        def lookup(kinds, table):
            result = jnp.zeros(kinds.shape, jnp.float32)
            for k in range(types):
                result = jnp.where(kinds == float(k), table[k], result)
            return result

        barrier = pltpu.get_barrier_semaphore()
        greeted = 0
        for axes, count in zip(groups, group_sizes):
            for hop in range(1, count):
                pl.semaphore_signal(
                    barrier, inc=1, device_id=member(axes, hop), device_id_type=MESH
                )
                greeted += 1
        if len(groups) > 1:
            for step in REMOTE:
                pl.semaphore_signal(
                    barrier, inc=1, device_id=neighbour(step), device_id_type=MESH
                )
                greeted += 1

        for load in loads:
            load.wait()

        def tenth(values, f, place):
            return (values + CELL_EDGE * (place[f] - 1.0)) * (1.0 / CUTOFF)

        def sigma(kinds):
            root = lax.rsqrt(lookup(kinds, gamma_ref))
            return root * root * root * (CUTOFF**-1.5)

        for x, y, z in local:
            for f in range(3):
                fields[x + 1, y + 1, z + 1, f : f + 1, :] = off_ref[f, x, y, z : z + 1, :]
            fields[x + 1, y + 1, z + 1, 3:4, :] = type_ref[x, y, z : z + 1, :].astype(jnp.float32)

        def locate(places):
            for x, y, z in places:
                place = (x, y, z)
                kinds = fields[x, y, z, 3:4, :]
                for f in range(3):
                    geometry[x, y, z, f : f + 1, :] = tenth(fields[x, y, z, f : f + 1, :], f, place)
                geometry[x, y, z, 3:4, :] = sigma(kinds)
                source[x, y, z, 0:1, :] = -lookup(kinds, chi_ref)
                source[x, y, z, 1:2, :] = jnp.full((1, atoms), -1.0, jnp.float32)

        locate([p for p in padded if reach(p) == 0])
        for t, (x, y, z) in enumerate(local):
            for f in range(4):
                row = geometry[x + 1, y + 1, z + 1, f : f + 1, :]
                columns[t, f] = jnp.transpose(jnp.broadcast_to(row, (atoms, atoms)))
        entries = jnp.concatenate(
            [list_ref[x, y, z : z + 1, :] - linear((x + 1, y + 1, z + 1)) for x, y, z in local], 0
        )
        for n, step in enumerate(STEPS):
            found = jnp.max(
                jnp.where(entries == linear(step), 1.0, 0.0), axis=1, keepdims=True
            )
            listed[n] = jnp.broadcast_to(1.0 - (1.0 - found) * FAR, (tiles, atoms))
        eta = [lookup(fields[x + 1, y + 1, z + 1, 3:4, :], eta_ref) for x, y, z in local]

        with jax.named_scope("barrier"):
            pl.semaphore_wait(barrier, greeted)

        def halo(buffer, stage):
            for step in REMOTE:
                here, there = rounded_sides(step, cells)
                kind = kind_of(step)
                pltpu.make_async_remote_copy(
                    src_ref=buffer.at[here],
                    dst_ref=buffer.at[there],
                    send_sem=halo_send.at[stage, kind],
                    recv_sem=halo_recv.at[stage, kind],
                    device_id=neighbour(step),
                    device_id_type=MESH,
                ).start()

        def whole_kind(buffer, stage, kind):
            return pltpu.make_async_remote_copy(
                src_ref=buffer.at[boxes[kind]],
                dst_ref=buffer.at[boxes[kind]],
                send_sem=halo_send.at[stage, kind],
                recv_sem=halo_recv.at[stage, kind],
                device_id=neighbour(REMOTE[0]),
                device_id_type=MESH,
            )

        def arrived(buffer, stage, which):
            if which == 1:
                whole_kind(buffer, stage, 0).wait_recv()
                whole_kind(buffer, stage, 1).wait_recv()
            if which == 2:
                whole_kind(buffer, stage, 2).wait_recv()

        slabs = atoms // rows

        def coupling(t, n, place, at, own_part):
            near = [geometry[place[0], place[1], place[2], f : f + 1, :] for f in range(4)]
            dx = near[0] - own_part[0]
            dy = near[1] - own_part[1]
            dz = near[2] - own_part[2]
            square = dx * dx + dy * dy + dz * dz
            if STEPS[n] == (0, 0, 0):
                i = lax.broadcasted_iota(jnp.int32, (rows, atoms), 0) + at
                j = lax.broadcasted_iota(jnp.int32, (rows, atoms), 1)
                square = jnp.where(i == j, 4.0, square)
            u = square * lax.rsqrt(square)
            w = jnp.maximum(listed[n, t : t + 1, :] - u, 0.0)
            w = w * w
            w = w * w
            shape = (u + 0.5) * (square + 0.2) - 0.05
            cube = square * u + own_part[3] * near[3]
            return w * shape * jnp.exp2(jnp.log2(cube) * (-1.0 / 3.0))

        def tile_pass(vector, which, building):
            def slab(index, carry):
                at = pl.multiple_of(index * rows, rows)
                for t, part in pairs[which]:
                    if which == 0:
                        total_s = jnp.zeros((rows, atoms), jnp.float32)
                        total_t = jnp.zeros((rows, atoms), jnp.float32)
                    else:
                        total_s = sums[t, 0, pl.ds(at, rows), :]
                        total_t = sums[t, 1, pl.ds(at, rows), :]
                    if building:
                        own_part = [columns[t, f, pl.ds(at, rows), :] for f in range(4)]
                    for n, place in part:
                        x, y, z = place
                        if building:
                            block = coupling(t, n, place, at, own_part)
                            blocks[t, n, pl.ds(at, rows), :] = block
                            total_t = total_t - block
                        else:
                            block = blocks[t, n, pl.ds(at, rows), :]
                            total_t = total_t + block * vector[x, y, z, 1:2, :]
                        total_s = total_s + block * vector[x, y, z, 0:1, :]
                    sums[t, 0, pl.ds(at, rows), :] = total_s
                    sums[t, 1, pl.ds(at, rows), :] = total_t
                return carry

            lax.fori_loop(0, slabs, slab, 0)

        scale = 20.0 * COULOMB / CUTOFF
        ones = jnp.ones((16, 3 * atoms), jnp.bfloat16)

        def collect(vector, image):
            for t, (x, y, z) in enumerate(local):
                for s in range(2):
                    left = sums[t, s]
                    pieces = []
                    for k in range(3):
                        piece = left.astype(jnp.bfloat16)
                        pieces.append(piece)
                        if k < 2:
                            left = left - piece.astype(jnp.float32)
                    row = lax.dot_general(
                        ones,
                        jnp.concatenate(pieces, axis=1),
                        (((1,), (1,)), ((), ())),
                        preferred_element_type=jnp.float32,
                    )[0:1]
                    here = vector[x + 1, y + 1, z + 1, s : s + 1, :]
                    image(x, y, z, s, eta[t] * here + scale * row)

        def to_padded(buffer):
            def store(x, y, z, s, row):
                buffer[x + 1, y + 1, z + 1, s : s + 1, :] = row

            return store

        def to_own(x, y, z, s, row):
            own_image[x, y, z, s : s + 1, :] = row

        lane = lax.broadcasted_iota(jnp.int32, (2, atoms), 1)

        def over_own(values):
            return jnp.sum(jnp.sum(values, axis=(0, 1, 2)), axis=1, keepdims=True)

        def sum_copies(g, stage):
            axes, count = groups[g], group_sizes[g]
            return [
                pltpu.make_async_remote_copy(
                    src_ref=parts[g].at[stage, 0],
                    dst_ref=parts[g].at[stage, hop],
                    send_sem=sum_send.at[stage, g],
                    recv_sem=sum_recv.at[stage, g],
                    device_id=member(axes, hop),
                    device_id_type=MESH,
                )
                for hop in range(1, count)
            ]

        def whole_sum(g, stage):
            count = group_sizes[g]
            return pltpu.make_async_remote_copy(
                src_ref=parts[g].at[stage, pl.ds(1, count - 1)],
                dst_ref=parts[g].at[stage, pl.ds(1, count - 1)],
                send_sem=sum_send.at[stage, g],
                recv_sem=sum_recv.at[stage, g],
                device_id=member(groups[g], 1),
                device_id_type=MESH,
            )

        def start_sums(values, stage):
            message = jnp.zeros((2, atoms), jnp.float32)
            for k, value in enumerate(values):
                message = jnp.where(lane == k, value, message)
            parts[0][stage, 0] = message
            for copy in sum_copies(0, stage):
                copy.start()

        def finish_sums(number, stage):
            for g in range(len(groups)):
                whole_sum(g, stage).wait_recv()
                total = jnp.sum(parts[g][stage], axis=0)
                if g + 1 < len(groups):
                    parts[g + 1][stage, 0] = total
                    for copy in sum_copies(g + 1, stage):
                        copy.start()
            return [
                jnp.sum(jnp.where(lane == k, total, 0.0), axis=1, keepdims=True)
                for k in range(number)
            ]

        halo(fields, 0)
        with jax.named_scope("build0"):
            tile_pass(source, 0, True)
        for which in (1, 2):
            with jax.named_scope(f"wait_pos{which}"):
                arrived(fields, 0, which)
            locate([p for p in padded if reach(p) == which])
            with jax.named_scope(f"build{which}"):
                tile_pass(source, which, True)
        with jax.named_scope("collect0"):
            collect(source, to_padded(first))

        def apply(vector, stage):
            with jax.named_scope(f"pass{stage}_0"):
                tile_pass(vector, 0, False)
            for which in (1, 2):
                with jax.named_scope(f"wait{stage}_{which}"):
                    arrived(vector, stage, which)
                with jax.named_scope(f"pass{stage}_{which}"):
                    tile_pass(vector, which, False)
            with jax.named_scope(f"collect{stage}"):
                collect(vector, to_own)

        halo(first, 1)
        residual = source[own]
        image = first[own]
        start_sums([over_own(residual * residual), over_own(residual * image)], 0)
        apply(first, 1)
        with jax.named_scope("sums0"):
            norm_now, curvature = finish_sums(2, 0)
        step_size = norm_now / curvature
        direction, along = residual, image
        further = own_image[...]
        answer = step_size * direction
        residual = residual - step_size * along
        image = image - step_size * further
        second[own] = image
        halo(second, 2)
        start_sums([over_own(residual * residual), over_own(residual * image)], 1)
        apply(second, 2)
        with jax.named_scope("sums1"):
            norm_next, curvature = finish_sums(2, 1)
        growth = norm_next / norm_now
        step_size = norm_next / (curvature - growth * norm_next / step_size)
        norm_now = norm_next
        further = own_image[...] + growth * further
        direction = residual + growth * direction
        along = image + growth * along
        answer = answer + step_size * direction
        residual = residual - step_size * along
        image = image - step_size * further
        values = [residual * residual, residual * image, answer, residual, direction]
        start_sums([over_own(v) for v in values], 2)
        with jax.named_scope("sums2"):
            norm_next, curvature, *others = finish_sums(5, 2)
        growth = norm_next / norm_now
        step_size = norm_next / (curvature - growth * norm_next / step_size)
        answer = answer + step_size * (residual + growth * direction)
        residual = residual - step_size * (image + growth * along)
        totals = others[0] + step_size * (others[1] + growth * others[2])
        level = totals[0:1] / totals[1:2]
        for x, y, z in local:
            charge_ref[x, y, z : z + 1, :] = 1000.0 * (
                answer[x, y, z, 0:1] - level * answer[x, y, z, 1:2]
            )
            for s in range(2):
                resid_ref[s, x, y, z : z + 1, :] = residual[x, y, z, s : s + 1]
        with jax.named_scope("drain"):
            for stage, buffer in enumerate((fields, first, second)):
                for kind in range(KINDS):
                    whole_kind(buffer, stage, kind).wait_send()
            for stage in range(ITERS):
                for g in range(len(groups)):
                    whole_sum(g, stage).wait_send()

    scratch = [
        pltpu.VMEM((3,) + cells + (atoms,), jnp.float32),
        pltpu.VMEM(cells + (atoms,), jnp.int32),
        None,
        pltpu.SMEM((types,), jnp.float32),
        pltpu.SMEM((types,), jnp.float32),
        pltpu.SMEM((types,), jnp.float32),
        pltpu.VMEM(width + (4, atoms), jnp.float32),
        pltpu.VMEM(width + (4, atoms), jnp.float32),
        pltpu.VMEM((tiles, 4, atoms, atoms), jnp.float32),
        pltpu.VMEM((len(STEPS), tiles, atoms), jnp.float32),
        pltpu.VMEM((tiles, len(STEPS), atoms, atoms), jnp.float32),
        pltpu.VMEM((tiles, 2, atoms, atoms), jnp.float32),
        pltpu.VMEM(width + (2, atoms), jnp.float32),
        pltpu.VMEM(width + (2, atoms), jnp.float32),
        pltpu.VMEM(width + (2, atoms), jnp.float32),
        pltpu.VMEM(cells + (2, atoms), jnp.float32),
    ]
    scratch += [pltpu.VMEM((ITERS, count, 2, atoms), jnp.float32) for count in group_sizes]
    scratch += [
        pltpu.SemaphoreType.DMA((6,)),
        pltpu.SemaphoreType.DMA((ITERS, KINDS)),
        pltpu.SemaphoreType.DMA((ITERS, KINDS)),
        pltpu.SemaphoreType.DMA((ITERS, len(groups))),
        pltpu.SemaphoreType.DMA((ITERS, len(groups))),
    ]
    return kernel, scratch


def solution(mesh):
    sizes = {a: mesh.shape[a] for a in AXES}
    devices = sizes["gx"] * sizes["gy"] * sizes["gz"]
    groups = (AXES,) if devices <= 64 else tuple((a,) for a in AXES)

    def per_device(offsets, type_ids, neighbours, type_chi, type_eta, type_gamma):
        cells = offsets.shape[1:4]
        atoms = offsets.shape[4]
        types = type_chi.shape[0]
        kernel, scratch = make_kernel(sizes, groups, cells, atoms, types, 32)
        scratch[2] = pltpu.VMEM(neighbours.shape, jnp.int32)
        vmem = pl.BlockSpec(memory_space=pltpu.VMEM)
        hbm = pl.BlockSpec(memory_space=pltpu.HBM)
        return pl.pallas_call(
            kernel,
            out_shape=(
                jax.ShapeDtypeStruct(cells + (atoms,), jnp.float32),
                jax.ShapeDtypeStruct((2,) + cells + (atoms,), jnp.float32),
            ),
            in_specs=[hbm] * 6,
            out_specs=(vmem, vmem),
            scratch_shapes=scratch,
            compiler_params=pltpu.CompilerParams(
                collective_id=0, has_side_effects=True, vmem_limit_bytes=48 * 1024 * 1024
            ),
        )(offsets, type_ids, neighbours, type_chi, type_eta, type_gamma)

    placed = (
        P(None, "gx", "gy", "gz", None),
        P("gx", "gy", "gz", None),
        P("gx", "gy", "gz", None),
        P(),
        P(),
        P(),
    )
    return jax.shard_map(
        per_device,
        mesh=mesh,
        in_specs=placed,
        out_specs=(P("gx", "gy", "gz", None), P(None, "gx", "gy", "gz", None)),
        check_vma=False,
    )
```

time: 49.5 us -> 37.2 us (0.75)
  Pallas kernels: 43.4 us -> 31.1 us
    pallas_call x1, Pallas kernels: 43.4 us -> 31.1 us  [per_device(): pl.pallas_call(kernel, out_shape=(jax.ShapeDtypeStruct(cells + (atoms,),...]
where the time goes in v1:
time: 37.2 us; the launch traced here: 36.9 us
  Pallas kernels  31.1 us (84%)
  local copies, waits for them, and re-layouts  5.18 us (14%)
  between operations  0.65 us (2%)
    pallas_call x1, Pallas kernels, per_device(): pl.pallas_call(kernel, out_shape=(jax.ShapeDtypeStruct(cells + (atoms,),...  31.1 us
    unnamed x14, local copies, waits for them, and re-layouts  5.18 us

profile of v1, /device:TPU:0, one launch (start us, length us, event | category | flops | bytes accessed | tf_op | source)
XLA Modules:
  0.0 36.9 jit_solution(2635177102852303801)
XLA Ops:
  0.6 0.0 copy-start
  0.6 0.7 %copy-done = f32[3,1,2,2,128]{4,3,2,1,0:T(2,128)S(1)} copy-done((f32[3,1,2,2,128]{4,3,2,1,0:T(2,128)S(1)}, f32[3,1,2,2,128]{4,3,2,1,0:T(2,128)}, u32[]{:S(2)}) %copy-start) | copy-done | bytes 6168
  1.3 0.0 copy-start.1
  1.3 0.7 %copy-done.1 = s32[1,2,2,128]{3,2,1,0:T(2,128)S(1)} copy-done((s32[1,2,2,128]{3,2,1,0:T(2,128)S(1)}, s32[1,2,2,128]{3,2,1,0:T(2,128)}, u32[]{:S(2)}) %copy-start.1) | copy-done | bytes 2072
  2.0 0.0 copy-start.2
  2.0 0.7 %copy-done.2 = s32[1,2,2,27]{3,2,1,0:T(2,128)S(1)} copy-done((s32[1,2,2,27]{3,2,1,0:T(2,128)S(1)}, s32[1,2,2,27]{3,2,1,0:T(2,128)}, u32[]{:S(2)}) %copy-start.2) | copy-done | bytes 456
  2.7 0.0 copy-start.3
  2.7 0.7 %copy-done.3 = f32[2]{0:T(128)S(1)} copy-done((f32[2]{0:T(128)S(1)}, f32[2]{0:T(128)}, u32[]{:S(2)}) %copy-start.3) | copy-done | bytes 32
  3.3 0.0 copy-start.4
  3.3 0.7 %copy-done.4 = f32[2]{0:T(128)S(1)} copy-done((f32[2]{0:T(128)S(1)}, f32[2]{0:T(128)}, u32[]{:S(2)}) %copy-start.4) | copy-done | bytes 32
  4.0 0.0 copy-start.5
  4.0 0.7 %copy-done.5 = f32[2]{0:T(128)S(1)} copy-done((f32[2]{0:T(128)S(1)}, f32[2]{0:T(128)}, u32[]{:S(2)}) %copy-start.5) | copy-done | bytes 32
  4.7 31.1 %shard_map.77 = (f32[1,2,2,128]{3,2,1,0:T(2,128)S(1)}, f32[2,1,2,2,128]{4,3,2,1,0:T(2,128)S(1)}) custom-call(f32[3,1,2,2,128]{4,3,2,1,0:T(2,128)S(1)} %copy-done, s32[1,2,2,128]{3,2,1,0:T(2,128)S(1)} %copy-done.1, s32[1,2,2,27]{3,2,1,0:T(2,128)S(1)} %copy-done.2, f32[2]{0:T(128)S(1)} %copy-done.3, f32[2]{0:T(128)S(1)} %copy-done.4, f32[2]{0:T(128)S(1)} %copy-done.5), custom_call_target="tpu_custom_call" | custom-call | tf_op jit(solution)/shard_map/pallas_call | solution.py:453
  35.8 0.6 %copy.10 = f32[1,2,2,128]{3,2,1,0:T(2,128)} copy(f32[1,2,2,128]{3,2,1,0:T(2,128)S(1)} %get-tuple-element.4) | data formatting | bytes 4096
  36.4 0.6 %copy.11 = f32[2,1,2,2,128]{4,3,2,1,0:T(2,128)} copy(f32[2,1,2,2,128]{4,3,2,1,0:T(2,128)S(1)} %get-tuple-element.5) | data formatting | bytes 8192
Async XLA Ops:
  0.6 0.7 %copy-start = (f32[3,1,2,2,128]{4,3,2,1,0:T(2,128)S(1)}, f32[3,1,2,2,128]{4,3,2,1,0:T(2,128)}, u32[]{:S(2)}) copy-start(f32[3,1,2,2,128]{4,3,2,1,0:T(2,128)} %refs_0_.1) | copy-start | bytes 18436
  1.3 0.7 %copy-start.1 = (s32[1,2,2,128]{3,2,1,0:T(2,128)S(1)}, s32[1,2,2,128]{3,2,1,0:T(2,128)}, u32[]{:S(2)}) copy-start(s32[1,2,2,128]{3,2,1,0:T(2,128)} %refs_1_.1) | copy-start | bytes 6148
  2.0 0.7 %copy-start.2 = (s32[1,2,2,27]{3,2,1,0:T(2,128)S(1)}, s32[1,2,2,27]{3,2,1,0:T(2,128)}, u32[]{:S(2)}) copy-start(s32[1,2,2,27]{3,2,1,0:T(2,128)} %refs_2_.1) | copy-start | bytes 1300
  2.7 0.7 %copy-start.3 = (f32[2]{0:T(128)S(1)}, f32[2]{0:T(128)}, u32[]{:S(2)}) copy-start(f32[2]{0:T(128)} %refs_3_.1) | copy-start | bytes 28
  3.3 0.7 %copy-start.4 = (f32[2]{0:T(128)S(1)}, f32[2]{0:T(128)}, u32[]{:S(2)}) copy-start(f32[2]{0:T(128)} %refs_4_.1) | copy-start | bytes 28
  4.0 0.7 %copy-start.5 = (f32[2]{0:T(128)S(1)}, f32[2]{0:T(128)}, u32[]{:S(2)}) copy-start(f32[2]{0:T(128)} %refs_5_.1) | copy-start | bytes 28

commit v2 on v1

--- a/solution.py
+++ b/solution.py
@@ -462,7 +462,7 @@
             compiler_params=pltpu.CompilerParams(
                 collective_id=0, has_side_effects=True, vmem_limit_bytes=48 * 1024 * 1024
             ),
-        )(offsets, type_ids, neighbours, type_chi, type_eta, type_gamma)
+        )(*[pltpu.with_memory_space_constraint(v, pltpu.HBM) for v in (offsets, type_ids, neighbours, type_chi, type_eta, type_gamma)])
 
     placed = (
         P(None, "gx", "gy", "gz", None),

time: 37.2 us -> 33.2 us (0.89)
  local copies, waits for them, and re-layouts: 5.18 us -> 1.17 us
    unnamed x14 -> x2, local copies, waits for them, and re-layouts: 5.18 us -> 1.17 us
where the time goes in v2:
time: 33.2 us; the launch traced here: 33 us
  Pallas kernels  31.2 us (94%)
  local copies, waits for them, and re-layouts  1.17 us (4%)
  between operations  0.64 us (2%)
    pallas_call x1, Pallas kernels, per_device(): pl.pallas_call(kernel, out_shape=(jax.ShapeDtypeStruct(cells + (atoms,),...  31.2 us
    unnamed x2, local copies, waits for them, and re-layouts  1.17 us

profile of v2, /device:TPU:0, one launch (start us, length us, event | category | flops | bytes accessed | tf_op | source)
XLA Modules:
  0.0 33.0 jit_solution(18336676529932972246)
XLA Ops:
  0.6 31.2 %shard_map.77 = (f32[1,2,2,128]{3,2,1,0:T(2,128)S(1)}, f32[2,1,2,2,128]{4,3,2,1,0:T(2,128)S(1)}) custom-call(f32[3,1,2,2,128]{4,3,2,1,0:T(2,128)} %refs_0_.1, s32[1,2,2,128]{3,2,1,0:T(2,128)} %refs_1_.1, s32[1,2,2,27]{3,2,1,0:T(2,128)} %refs_2_.1, f32[2]{0:T(128)} %refs_3_.1, f32[2]{0:T(128)} %refs_4_.1, f32[2]{0:T(128)} %refs_5_.1), custom_call_target="tpu_custom_call" | custom-call | tf_op jit(solution)/shard_map/pallas_call | solution.py:453
  31.9 0.6 %copy.10 = f32[1,2,2,128]{3,2,1,0:T(2,128)} copy(f32[1,2,2,128]{3,2,1,0:T(2,128)S(1)} %get-tuple-element.4) | data formatting | bytes 4096
  32.4 0.6 %copy.11 = f32[2,1,2,2,128]{4,3,2,1,0:T(2,128)} copy(f32[2,1,2,2,128]{4,3,2,1,0:T(2,128)S(1)} %get-tuple-element.5) | data formatting | bytes 8192

commit v3 on v2

--- a/solution.py
+++ b/solution.py
@@ -76,9 +76,10 @@
     def kernel(*refs):
         hbm, (charge_ref, resid_ref) = refs[:6], refs[6:8]
         (off_ref, type_ref, list_ref, chi_ref, eta_ref, gamma_ref) = refs[8:14]
-        (fields, geometry, columns, listed, blocks, sums, source, first, second, own_image) = refs[14:24]
-        parts = refs[24 : 24 + len(groups)]
-        load_sem, halo_send, halo_recv, sum_send, sum_recv = refs[24 + len(groups) :]
+        (fields, geometry, shields, columns, listed, blocks, sums, source) = refs[14:22]
+        (first, second, own_image) = refs[22:25]
+        parts = refs[25 : 25 + len(groups)]
+        load_sem, halo_send, halo_recv, sum_send, sum_recv = refs[25 + len(groups) :]
 
         loads = [
             pltpu.make_async_copy(a, b, load_sem.at[k])
@@ -86,9 +87,6 @@
                 zip(hbm, (off_ref, type_ref, list_ref, chi_ref, eta_ref, gamma_ref))
             )
         ]
-        for load in loads:
-            load.start()
-
         me = {a: lax.axis_index(a) for a in AXES}
 
         def neighbour(step):
@@ -115,6 +113,8 @@
                 result = jnp.where(kinds == float(k), table[k], result)
             return result
 
+        for load in loads[:2]:
+            load.start()
         barrier = pltpu.get_barrier_semaphore()
         greeted = 0
         for axes, count in zip(groups, group_sizes):
@@ -130,11 +130,29 @@
                 )
                 greeted += 1
 
-        for load in loads:
+        for load in loads[2:]:
+            load.start()
+        for load in loads[:2]:
             load.wait()
 
-        def tenth(values, f, place):
-            return (values + CELL_EDGE * (place[f] - 1.0)) * (1.0 / CUTOFF)
+        row4 = lax.broadcasted_iota(jnp.int32, (4, atoms), 0)
+
+        def shifted(place):
+            parts = [CELL_EDGE * (p - 1.0 - 0.5 * c) for p, c in zip(place, cells)]
+            return jnp.where(row4 == 0, parts[0], jnp.where(row4 == 1, parts[1], parts[2]))
+
+        def stacked(raw, place):
+            p = jnp.where(row4 < 3, (raw + shifted(place)) * (1.0 / CUTOFF), 0.0)
+            return jnp.where(row4 < 3, p, jnp.sum(p * p, axis=0, keepdims=True))
+
+        def thirds(values):
+            pieces = []
+            for k in range(3):
+                piece = values.astype(jnp.bfloat16).astype(jnp.float32)
+                pieces.append(piece)
+                if k < 2:
+                    values = values - piece
+            return pieces
 
         def sigma(kinds):
             root = lax.rsqrt(lookup(kinds, gamma_ref))
@@ -149,26 +167,14 @@
             for x, y, z in places:
                 place = (x, y, z)
                 kinds = fields[x, y, z, 3:4, :]
-                for f in range(3):
-                    geometry[x, y, z, f : f + 1, :] = tenth(fields[x, y, z, f : f + 1, :], f, place)
-                geometry[x, y, z, 3:4, :] = sigma(kinds)
+                v1, v2, v3 = thirds(stacked(fields[x, y, z], place))
+                unit = jnp.where(row4 < 3, 1.0, 0.0)
+                geometry[x, y, z] = jnp.concatenate(
+                    [v1, v2, v3, v1, v2, v1, unit, jnp.zeros_like(unit)], axis=0
+                )
+                shields[x, y, z, 0:1, :] = sigma(kinds)
                 source[x, y, z, 0:1, :] = -lookup(kinds, chi_ref)
                 source[x, y, z, 1:2, :] = jnp.full((1, atoms), -1.0, jnp.float32)
-
-        locate([p for p in padded if reach(p) == 0])
-        for t, (x, y, z) in enumerate(local):
-            for f in range(4):
-                row = geometry[x + 1, y + 1, z + 1, f : f + 1, :]
-                columns[t, f] = jnp.transpose(jnp.broadcast_to(row, (atoms, atoms)))
-        entries = jnp.concatenate(
-            [list_ref[x, y, z : z + 1, :] - linear((x + 1, y + 1, z + 1)) for x, y, z in local], 0
-        )
-        for n, step in enumerate(STEPS):
-            found = jnp.max(
-                jnp.where(entries == linear(step), 1.0, 0.0), axis=1, keepdims=True
-            )
-            listed[n] = jnp.broadcast_to(1.0 - (1.0 - found) * FAR, (tiles, atoms))
-        eta = [lookup(fields[x + 1, y + 1, z + 1, 3:4, :], eta_ref) for x, y, z in local]
 
         with jax.named_scope("barrier"):
             pl.semaphore_wait(barrier, greeted)
@@ -206,11 +212,12 @@
         slabs = atoms // rows
 
         def coupling(t, n, place, at, own_part):
-            near = [geometry[place[0], place[1], place[2], f : f + 1, :] for f in range(4)]
-            dx = near[0] - own_part[0]
-            dy = near[1] - own_part[1]
-            dz = near[2] - own_part[2]
-            square = dx * dx + dy * dy + dz * dz
+            square = lax.dot_general(
+                own_part[0][:, :32],
+                geometry[place],
+                (((1,), (0,)), ((), ())),
+                preferred_element_type=jnp.float32,
+            )
             if STEPS[n] == (0, 0, 0):
                 i = lax.broadcasted_iota(jnp.int32, (rows, atoms), 0) + at
                 j = lax.broadcasted_iota(jnp.int32, (rows, atoms), 1)
@@ -220,7 +227,7 @@
             w = w * w
             w = w * w
             shape = (u + 0.5) * (square + 0.2) - 0.05
-            cube = square * u + own_part[3] * near[3]
+            cube = square * u + own_part[1] * shields[place[0], place[1], place[2], 0:1, :]
             return w * shape * jnp.exp2(jnp.log2(cube) * (-1.0 / 3.0))
 
         def tile_pass(vector, which, building):
@@ -234,7 +241,7 @@
                         total_s = sums[t, 0, pl.ds(at, rows), :]
                         total_t = sums[t, 1, pl.ds(at, rows), :]
                     if building:
-                        own_part = [columns[t, f, pl.ds(at, rows), :] for f in range(4)]
+                        own_part = [columns[t, f, pl.ds(at, rows), :] for f in range(2)]
                     for n, place in part:
                         x, y, z = place
                         if building:
@@ -334,6 +341,34 @@
             ]
 
         halo(fields, 0)
+        for load in loads[2:]:
+            load.wait()
+        locate([p for p in padded if reach(p) == 0])
+        for t, (x, y, z) in enumerate(local):
+            place = (x + 1, y + 1, z + 1)
+            v1, v2, v3 = thirds(stacked(fields[place], place))
+            c1 = jnp.where(row4 < 3, -2.0 * v1, 1.0)
+            c2 = jnp.where(row4 < 3, -2.0 * v2, 0.0)
+            c3 = jnp.where(row4 < 3, -2.0 * v3, 0.0)
+            norms = jnp.where(
+                row4 == 0, v1[3:4], jnp.where(row4 == 1, v2[3:4], jnp.where(row4 == 2, v3[3:4], 0.0))
+            )
+            none = jnp.zeros((atoms - 28, atoms), jnp.float32)
+            columns[t, 0] = jnp.transpose(
+                jnp.concatenate([c1, c1, c1, c2, c2, c3, norms, none], axis=0)
+            )
+            row = shields[x + 1, y + 1, z + 1, 0:1, :]
+            columns[t, 1] = jnp.transpose(jnp.broadcast_to(row, (atoms, atoms)))
+        entries = jnp.concatenate(
+            [list_ref[x, y, z : z + 1, :] - linear((x + 1, y + 1, z + 1)) for x, y, z in local], 0
+        )
+        for n, step in enumerate(STEPS):
+            found = jnp.max(
+                jnp.where(entries == linear(step), 1.0, 0.0), axis=1, keepdims=True
+            )
+            listed[n] = jnp.broadcast_to(1.0 - (1.0 - found) * FAR, (tiles, atoms))
+        eta = [lookup(fields[x + 1, y + 1, z + 1, 3:4, :], eta_ref) for x, y, z in local]
+
         with jax.named_scope("build0"):
             tile_pass(source, 0, True)
         for which in (1, 2):
@@ -416,8 +451,9 @@
         pltpu.SMEM((types,), jnp.float32),
         pltpu.SMEM((types,), jnp.float32),
         pltpu.VMEM(width + (4, atoms), jnp.float32),
-        pltpu.VMEM(width + (4, atoms), jnp.float32),
-        pltpu.VMEM((tiles, 4, atoms, atoms), jnp.float32),
+        pltpu.VMEM(width + (32, atoms), jnp.float32),
+        pltpu.VMEM(width + (1, atoms), jnp.float32),
+        pltpu.VMEM((tiles, 2, atoms, atoms), jnp.float32),
         pltpu.VMEM((len(STEPS), tiles, atoms), jnp.float32),
         pltpu.VMEM((tiles, len(STEPS), atoms, atoms), jnp.float32),
         pltpu.VMEM((tiles, 2, atoms, atoms), jnp.float32),
@@ -437,6 +473,17 @@
     return kernel, scratch
 
 
+def put_out(charge_in, resid_in, charge_ref, resid_ref, sems):
+    copies = [
+        pltpu.make_async_copy(charge_in, charge_ref, sems.at[0]),
+        pltpu.make_async_copy(resid_in, resid_ref, sems.at[1]),
+    ]
+    for copy in copies:
+        copy.start()
+    for copy in copies:
+        copy.wait()
+
+
 def solution(mesh):
     sizes = {a: mesh.shape[a] for a in AXES}
     devices = sizes["gx"] * sizes["gy"] * sizes["gz"]
@@ -446,11 +493,11 @@
         cells = offsets.shape[1:4]
         atoms = offsets.shape[4]
         types = type_chi.shape[0]
-        kernel, scratch = make_kernel(sizes, groups, cells, atoms, types, 32)
+        kernel, scratch = make_kernel(sizes, groups, cells, atoms, types, 128)
         scratch[2] = pltpu.VMEM(neighbours.shape, jnp.int32)
         vmem = pl.BlockSpec(memory_space=pltpu.VMEM)
         hbm = pl.BlockSpec(memory_space=pltpu.HBM)
-        return pl.pallas_call(
+        pair = pl.pallas_call(
             kernel,
             out_shape=(
                 jax.ShapeDtypeStruct(cells + (atoms,), jnp.float32),
@@ -463,6 +510,13 @@
                 collective_id=0, has_side_effects=True, vmem_limit_bytes=48 * 1024 * 1024
             ),
         )(*[pltpu.with_memory_space_constraint(v, pltpu.HBM) for v in (offsets, type_ids, neighbours, type_chi, type_eta, type_gamma)])
+        return pl.pallas_call(
+            put_out,
+            out_shape=tuple(jax.ShapeDtypeStruct(v.shape, v.dtype) for v in pair),
+            in_specs=[vmem] * 2,
+            out_specs=(hbm, hbm),
+            scratch_shapes=[pltpu.SemaphoreType.DMA((2,))],
+        )(*[pltpu.with_memory_space_constraint(v, pltpu.VMEM) for v in pair])
 
     placed = (
         P(None, "gx", "gy", "gz", None),

time: 33.2 us -> 31.1 us (0.937)
  local copies, waits for them, and re-layouts: 1.17 us -> 0 us
  Pallas kernels: 31.2 us -> 30.3 us
    pallas_call x1, Pallas kernels: 31.2 us -> 29.7 us  [per_device(): pl.pallas_call(kernel, out_shape=(jax.ShapeDtypeStruct(cells + (atoms,),...]
    unnamed x2 -> x0, local copies, waits for them, and re-layouts: 1.17 us -> none
    pallas_call x0 -> x1, Pallas kernels: none -> 0.62 us  [per_device(): pl.pallas_call(put_out, out_shape=tuple((jax.ShapeDtypeStruct(v.shape, v....]
where the time goes in v3:
time: 31.1 us; the launch traced here: 31 us
  Pallas kernels  30.3 us (97%)
  between operations  0.64 us (2%)
    pallas_call x1, Pallas kernels, per_device(): pl.pallas_call(kernel, out_shape=(jax.ShapeDtypeStruct(cells + (atoms,),...  29.7 us

profile of v3, /device:TPU:0, one launch (start us, length us, event | category | flops | bytes accessed | tf_op | source)
XLA Modules:
  0.0 31.0 jit_solution(8014851535776946068)
XLA Ops:
  0.6 29.7 %shard_map.77 = (f32[1,2,2,128]{3,2,1,0:T(2,128)S(1)}, f32[2,1,2,2,128]{4,3,2,1,0:T(2,128)S(1)}) custom-call(f32[3,1,2,2,128]{4,3,2,1,0:T(2,128)} %refs_0_.1, s32[1,2,2,128]{3,2,1,0:T(2,128)} %refs_1_.1, s32[1,2,2,27]{3,2,1,0:T(2,128)} %refs_2_.1, f32[2]{0:T(128)} %refs_3_.1, f32[2]{0:T(128)} %refs_4_.1, f32[2]{0:T(128)} %refs_5_.1), custom_call_target="tpu_custom_call" | custom-call | tf_op jit(solution)/shard_map/pallas_call | solution.py:500
  30.4 0.6 %shard_map.78 = (f32[1,2,2,128]{3,2,1,0:T(2,128)}, f32[2,1,2,2,128]{4,3,2,1,0:T(2,128)}) custom-call(f32[1,2,2,128]{3,2,1,0:T(2,128)S(1)} %get-tuple-element.4.charge_in, f32[2,1,2,2,128]{4,3,2,1,0:T(2,128)S(1)} %get-tuple-element.5.resid_in), custom_call_target="tpu_custom_call" | custom-call | tf_op jit(solution)/shard_map/pallas_call | solution.py:513

commit v4 on v3

--- a/solution.py
+++ b/solution.py
@@ -16,11 +16,9 @@
 MESH = pl.DeviceIdType.MESH
 STEPS = [d for d in itertools.product((-1, 0, 1), repeat=3)]
 REMOTE = sorted((d for d in STEPS if d != (0, 0, 0)), key=lambda d: (-abs(d[2]), -abs(d[0])))
-KINDS = 3
-
-
-def kind_of(step):
-    return 2 if step[2] else (1 if step[0] else 0)
+DISTANT = [d for d in REMOTE if d[2]]
+CLOSE = [d for d in REMOTE if not d[2]]
+KINDS = 6
 
 
 def rounded_sides(step, cells):
@@ -52,26 +50,28 @@
         group_sizes.append(count)
     boxes = (
         (pl.ds(0, cells[0]), pl.ds(0, 2), pl.ds(0, cells[2])),
-        (pl.ds(0, 2), pl.ds(0, width[1]), pl.ds(0, cells[2])),
-        (pl.ds(0, width[0]), pl.ds(0, width[1]), pl.ds(0, 2)),
+        (pl.ds(0, 2), pl.ds(0, 2), pl.ds(0, cells[2])),
+        (pl.ds(0, width[0]), pl.ds(0, width[1]), pl.ds(0, 1)),
+        (pl.ds(0, 1), pl.ds(0, cells[1]), pl.ds(0, cells[2])),
+        (pl.ds(0, 1), pl.ds(0, cells[1]), pl.ds(0, cells[2])),
+        (pl.ds(0, width[0]), pl.ds(0, width[1]), pl.ds(0, 1)),
     )
+    paired = cells[0] == 1 and sizes["gx"] % 2 == 0
+    planes = paired and len(groups) == 1
+    base = atoms // (2 * tiles)
 
     def linear(place):
         return (place[0] * width[1] + place[1]) * width[2] + place[2]
 
+    def inside(place, axes):
+        return all(1 <= place[a] <= cells[a] for a in axes)
+
     def reach(place):
-        if not 1 <= place[2] <= cells[2]:
-            return 2
-        return 0 if all(1 <= p <= c for p, c in zip(place, cells)) else 1
-
-    pairs = [[], [], []]
-    for t, home in enumerate(local):
-        split = [[], [], []]
-        for n, step in enumerate(STEPS):
-            place = tuple(h + 1 + d for h, d in zip(home, step))
-            split[reach(place)].append((n, place))
-        for kept, part in zip(pairs, split):
-            kept.append((t, part))
+        if inside(place, (0, 1, 2)):
+            return 0
+        if not inside(place, (2,)):
+            return 3
+        return 1 if paired and inside(place, (1,)) and place[0] == 0 else 2
 
     def kernel(*refs):
         hbm, (charge_ref, resid_ref) = refs[:6], refs[6:8]
@@ -79,7 +79,7 @@
         (fields, geometry, shields, columns, listed, blocks, sums, source) = refs[14:22]
         (first, second, own_image) = refs[22:25]
         parts = refs[25 : 25 + len(groups)]
-        load_sem, halo_send, halo_recv, sum_send, sum_recv = refs[25 + len(groups) :]
+        load_sem, halo_send, halo_recv, sum_send, sum_recv, met = refs[25 + len(groups) :]
 
         loads = [
             pltpu.make_async_copy(a, b, load_sem.at[k])
@@ -88,6 +88,58 @@
             )
         ]
         me = {a: lax.axis_index(a) for a in AXES}
+        side = 2 * (1 - lax.rem(me["gx"], 2)) if paired else 0
+
+        def real(place):
+            if paired and inside(place, (1, 2)) and place[0] != 1:
+                return (side if place[0] == 0 else 2 - side,) + place[1:]
+            return place
+
+        def arrival(step):
+            if step[2] > 0:
+                return jnp.where(me["gz"] == sizes["gz"] - 1, 5, 2)
+            if step[2] < 0:
+                return jnp.where(me["gz"] == 1, 2, 5)
+            if step[1]:
+                return 1 if step[0] else 0
+            if not paired:
+                return 3 if step[0] > 0 else 4
+            return jnp.where(side - 1 == step[0], 3, 4)
+
+        def departure(step):
+            if step[2]:
+                return 2 if step[2] > 0 else 5
+            if step[1]:
+                return 1 if step[0] else 0
+            return 3 if step[0] > 0 else 4
+
+        pairs = [[] for _ in range(5)]
+        for t, home in enumerate(local):
+            split = [[], [], []]
+            for step in STEPS:
+                marked = tuple(h + 1 + d for h, d in zip(home, step))
+                if reach(marked) == 3:
+                    continue
+                place = real(marked)
+                n = ((place[0] - home[0]) * 3 + step[1] + 1) * 3 + step[2] + 1
+                split[reach(marked)].append((n, place, step == (0, 0, 0)))
+            for kept, part in zip(pairs, split):
+                kept.append((t, part))
+        edge = me["gz"] == 0
+        far = (jnp.where(edge, cells[2] + 1, 0), jnp.where(edge, 0, cells[2] + 1))
+        for which, pz in zip((3, 4), far):
+            tz = jnp.where(pz == 0, 0, cells[2] - 1)
+            for x, y in itertools.product(range(cells[0]), range(cells[1])):
+                part = [
+                    ((a * 3 + b) * 3 + pz - tz, (x + a, y + b, pz), False)
+                    for a, b in itertools.product(range(3), repeat=2)
+                ]
+                pairs[which].append(((x * cells[1] + y) * cells[2] + tz, part))
+
+        def places_of(which):
+            if which < 3:
+                return [real(p) for p in padded if reach(p) == which]
+            return [p + (far[which - 3],) for p in itertools.product(*map(range, width[:2]))]
 
         def neighbour(step):
             return tuple(
@@ -116,19 +168,58 @@
         for load in loads[:2]:
             load.start()
         barrier = pltpu.get_barrier_semaphore()
+
+        def greet(place):
+            pl.semaphore_signal(barrier, inc=1, device_id=place, device_id_type=MESH)
+
+        odd = lax.rem(me["gx"], 2)
         greeted = 0
-        for axes, count in zip(groups, group_sizes):
-            for hop in range(1, count):
-                pl.semaphore_signal(
-                    barrier, inc=1, device_id=member(axes, hop), device_id_type=MESH
-                )
-                greeted += 1
-        if len(groups) > 1:
-            for step in REMOTE:
-                pl.semaphore_signal(
-                    barrier, inc=1, device_id=neighbour(step), device_id_type=MESH
-                )
-                greeted += 1
+        if planes:
+            for dz in range(sizes["gz"]):
+                for k, dy in itertools.product(range(sizes["gx"] // 2), range(sizes["gy"])):
+                    x = me["gx"] - odd + 2 * k + (1 if dz else 0)
+                    place = (
+                        lax.rem(x, sizes["gx"]),
+                        lax.rem(me["gy"] + dy, sizes["gy"]),
+                        lax.rem(me["gz"] + dz, sizes["gz"]),
+                    )
+                    if (dz, k, dy) == (0, 0, 0):
+                        pl.when(odd == 1)(lambda place=place: greet(place))
+                    else:
+                        greet(place)
+        else:
+            for axes, count in zip(groups, group_sizes):
+                for hop in range(1, count):
+                    greet(member(axes, hop))
+                    greeted += 1
+            if len(groups) > 1:
+                for step in REMOTE:
+                    greet(neighbour(step))
+                    greeted += 1
+
+        def tell(which):
+            partner = (me["gx"] + 1 - 2 * odd, me["gy"], me["gz"])
+            pl.semaphore_signal(met.at[which], inc=1, device_id=partner, device_id_type=MESH)
+
+        def plane_is_in():
+            @pl.when(odd == 0)
+            def _():
+                pl.semaphore_wait(barrier, sizes["gx"] * sizes["gy"] - 1)
+                tell(0)
+
+            @pl.when(odd == 1)
+            def _():
+                pl.semaphore_wait(met.at[0], 1)
+
+        def others_are_in():
+            @pl.when(odd == 1)
+            def _():
+                pl.semaphore_wait(barrier, sizes["gx"] * sizes["gy"] * (sizes["gz"] - 1))
+                tell(1)
+
+            @pl.when(odd == 0)
+            def _():
+                pl.semaphore_wait(met.at[1], 1)
 
         for load in loads[2:]:
             load.start()
@@ -138,8 +229,11 @@
         row4 = lax.broadcasted_iota(jnp.int32, (4, atoms), 0)
 
         def shifted(place):
-            parts = [CELL_EDGE * (p - 1.0 - 0.5 * c) for p, c in zip(place, cells)]
-            return jnp.where(row4 == 0, parts[0], jnp.where(row4 == 1, parts[1], parts[2]))
+            ends = [
+                CELL_EDGE * (jnp.asarray(p, jnp.int32).astype(jnp.float32) - (1.0 + 0.5 * c))
+                for p, c in zip(place, cells)
+            ]
+            return jnp.where(row4 == 0, ends[0], jnp.where(row4 == 1, ends[1], ends[2]))
 
         def stacked(raw, place):
             p = jnp.where(row4 < 3, (raw + shifted(place)) * (1.0 / CUTOFF), 0.0)
@@ -164,8 +258,8 @@
             fields[x + 1, y + 1, z + 1, 3:4, :] = type_ref[x, y, z : z + 1, :].astype(jnp.float32)
 
         def locate(places):
-            for x, y, z in places:
-                place = (x, y, z)
+            for place in places:
+                x, y, z = place
                 kinds = fields[x, y, z, 3:4, :]
                 v1, v2, v3 = thirds(stacked(fields[x, y, z], place))
                 unit = jnp.where(row4 < 3, 1.0, 0.0)
@@ -177,17 +271,19 @@
                 source[x, y, z, 1:2, :] = jnp.full((1, atoms), -1.0, jnp.float32)
 
         with jax.named_scope("barrier"):
-            pl.semaphore_wait(barrier, greeted)
-
-        def halo(buffer, stage):
-            for step in REMOTE:
+            if planes:
+                plane_is_in()
+            else:
+                pl.semaphore_wait(barrier, greeted)
+
+        def halo(buffer, stage, steps=REMOTE):
+            for step in steps:
                 here, there = rounded_sides(step, cells)
-                kind = kind_of(step)
                 pltpu.make_async_remote_copy(
                     src_ref=buffer.at[here],
                     dst_ref=buffer.at[there],
-                    send_sem=halo_send.at[stage, kind],
-                    recv_sem=halo_recv.at[stage, kind],
+                    send_sem=halo_send.at[stage, departure(step)],
+                    recv_sem=halo_recv.at[stage, arrival(step)],
                     device_id=neighbour(step),
                     device_id_type=MESH,
                 ).start()
@@ -203,38 +299,45 @@
             )
 
         def arrived(buffer, stage, which):
-            if which == 1:
-                whole_kind(buffer, stage, 0).wait_recv()
-                whole_kind(buffer, stage, 1).wait_recv()
-            if which == 2:
-                whole_kind(buffer, stage, 2).wait_recv()
-
-        slabs = atoms // rows
-
-        def coupling(t, n, place, at, own_part):
+            for kind in ((), (3,), (0, 1, 4) if paired else (0, 1, 3, 4), (2,), (5,))[which]:
+                whole_kind(buffer, stage, kind).wait_recv()
+
+        def coupling(t, n, place, at, own_part, itself):
             square = lax.dot_general(
                 own_part[0][:, :32],
                 geometry[place],
                 (((1,), (0,)), ((), ())),
                 preferred_element_type=jnp.float32,
             )
-            if STEPS[n] == (0, 0, 0):
+            if itself:
                 i = lax.broadcasted_iota(jnp.int32, (rows, atoms), 0) + at
                 j = lax.broadcasted_iota(jnp.int32, (rows, atoms), 1)
                 square = jnp.where(i == j, 4.0, square)
             u = square * lax.rsqrt(square)
-            w = jnp.maximum(listed[n, t : t + 1, :] - u, 0.0)
+            w = jnp.maximum(listed[n, pl.ds(t, 1), :] - u, 0.0)
             w = w * w
             w = w * w
             shape = (u + 0.5) * (square + 0.2) - 0.05
             cube = square * u + own_part[1] * shields[place[0], place[1], place[2], 0:1, :]
             return w * shape * jnp.exp2(jnp.log2(cube) * (-1.0 / 3.0))
 
-        def tile_pass(vector, which, building):
+        lanes = lax.broadcasted_iota(jnp.int32, (rows, atoms), 1)
+
+        def fold(first_half, second_half, shift):
+            clear = (lanes & shift) == 0
+            kept = jnp.where(clear, first_half, second_half)
+            return kept + pltpu.roll(jnp.where(clear, second_half, first_half), shift, 1)
+
+        def tile_pass(vector, groups_now, building):
+            merged = [(t, list(part)) for t, part in pairs[groups_now[0]]]
+            for which in groups_now[1:]:
+                for (_, kept), (_, part) in zip(merged, pairs[which]):
+                    kept.extend(part)
+
             def slab(index, carry):
                 at = pl.multiple_of(index * rows, rows)
-                for t, part in pairs[which]:
-                    if which == 0:
+                for t, part in merged:
+                    if 0 in groups_now:
                         total_s = jnp.zeros((rows, atoms), jnp.float32)
                         total_t = jnp.zeros((rows, atoms), jnp.float32)
                     else:
@@ -242,10 +345,9 @@
                         total_t = sums[t, 1, pl.ds(at, rows), :]
                     if building:
                         own_part = [columns[t, f, pl.ds(at, rows), :] for f in range(2)]
-                    for n, place in part:
-                        x, y, z = place
+                    for n, (x, y, z), itself in part:
                         if building:
-                            block = coupling(t, n, place, at, own_part)
+                            block = coupling(t, n, (x, y, z), at, own_part, itself)
                             blocks[t, n, pl.ds(at, rows), :] = block
                             total_t = total_t - block
                         else:
@@ -256,38 +358,49 @@
                     sums[t, 1, pl.ds(at, rows), :] = total_t
                 return carry
 
-            lax.fori_loop(0, slabs, slab, 0)
+            lax.fori_loop(0, atoms // rows, slab, 0)
 
         scale = 20.0 * COULOMB / CUTOFF
-        ones = jnp.ones((16, 3 * atoms), jnp.bfloat16)
+        high = max(16, 2 * tiles)
+        sheaf = lax.broadcasted_iota(jnp.int32, (high, 3 * atoms), 1) % atoms // base
+        gather = jnp.where(
+            sheaf == lax.broadcasted_iota(jnp.int32, (high, 3 * atoms), 0), 1.0, 0.0
+        ).astype(jnp.bfloat16)
 
         def collect(vector, image):
+            folded = []
+            for at in range(0, atoms, rows):
+                left = [sums[t, k, at : at + rows, :] for t in range(tiles) for k in range(2)]
+                shift = base
+                while len(left) > 1:
+                    left = [fold(a, b, shift) for a, b in zip(left[::2], left[1::2])]
+                    shift = 2 * shift
+                folded.append(left[0])
+            left = jnp.concatenate(folded, axis=0)
+            pieces = []
+            for k in range(3):
+                piece = left.astype(jnp.bfloat16)
+                pieces.append(piece)
+                if k < 2:
+                    left = left - piece.astype(jnp.float32)
+            result = lax.dot_general(
+                gather,
+                jnp.concatenate(pieces, axis=1),
+                (((1,), (1,)), ((), ())),
+                preferred_element_type=jnp.float32,
+            )
             for t, (x, y, z) in enumerate(local):
-                for s in range(2):
-                    left = sums[t, s]
-                    pieces = []
-                    for k in range(3):
-                        piece = left.astype(jnp.bfloat16)
-                        pieces.append(piece)
-                        if k < 2:
-                            left = left - piece.astype(jnp.float32)
-                    row = lax.dot_general(
-                        ones,
-                        jnp.concatenate(pieces, axis=1),
-                        (((1,), (1,)), ((), ())),
-                        preferred_element_type=jnp.float32,
-                    )[0:1]
-                    here = vector[x + 1, y + 1, z + 1, s : s + 1, :]
-                    image(x, y, z, s, eta[t] * here + scale * row)
+                here = vector[x + 1, y + 1, z + 1]
+                image(x, y, z, eta[t] * here + scale * result[2 * t : 2 * t + 2])
 
         def to_padded(buffer):
-            def store(x, y, z, s, row):
-                buffer[x + 1, y + 1, z + 1, s : s + 1, :] = row
+            def store(x, y, z, pair):
+                buffer[x + 1, y + 1, z + 1] = pair
 
             return store
 
-        def to_own(x, y, z, s, row):
-            own_image[x, y, z, s : s + 1, :] = row
+        def to_own(x, y, z, pair):
+            own_image[x, y, z] = pair
 
         lane = lax.broadcasted_iota(jnp.int32, (2, atoms), 1)
 
@@ -340,10 +453,19 @@
                 for k in range(number)
             ]
 
-        halo(fields, 0)
+        def distant_positions():
+            others_are_in()
+            halo(fields, 0, DISTANT)
+
+        last = me["gz"] == sizes["gz"] - 1
+        if planes:
+            halo(fields, 0, CLOSE)
+            pl.when(last)(distant_positions)
+        else:
+            halo(fields, 0)
         for load in loads[2:]:
             load.wait()
-        locate([p for p in padded if reach(p) == 0])
+        locate(places_of(0))
         for t, (x, y, z) in enumerate(local):
             place = (x + 1, y + 1, z + 1)
             v1, v2, v3 = thirds(stacked(fields[place], place))
@@ -370,34 +492,45 @@
         eta = [lookup(fields[x + 1, y + 1, z + 1, 3:4, :], eta_ref) for x, y, z in local]
 
         with jax.named_scope("build0"):
-            tile_pass(source, 0, True)
-        for which in (1, 2):
+            tile_pass(source, (0,), True)
+        for which in (1, 2, 3, 4) if paired else (2, 3, 4):
+            if which == 2 and planes:
+                with jax.named_scope("others"):
+                    pl.when(jnp.logical_not(last))(distant_positions)
             with jax.named_scope(f"wait_pos{which}"):
                 arrived(fields, 0, which)
-            locate([p for p in padded if reach(p) == which])
+            locate(places_of(which))
             with jax.named_scope(f"build{which}"):
-                tile_pass(source, which, True)
+                tile_pass(source, (which,), True)
         with jax.named_scope("collect0"):
             collect(source, to_padded(first))
 
-        def apply(vector, stage):
+        def apply(vector, stage, number):
             with jax.named_scope(f"pass{stage}_0"):
-                tile_pass(vector, 0, False)
-            for which in (1, 2):
+                tile_pass(vector, (0,), False)
+            with jax.named_scope(f"wait{stage}_1"):
+                if paired:
+                    arrived(vector, stage, 1)
+                arrived(vector, stage, 2)
+            with jax.named_scope(f"pass{stage}_1"):
+                tile_pass(vector, (1, 2) if paired else (2,), False)
+            for which in (3, 4):
                 with jax.named_scope(f"wait{stage}_{which}"):
                     arrived(vector, stage, which)
                 with jax.named_scope(f"pass{stage}_{which}"):
-                    tile_pass(vector, which, False)
-            with jax.named_scope(f"collect{stage}"):
-                collect(vector, to_own)
-
-        halo(first, 1)
+                    tile_pass(vector, (which,), False)
+            with jax.named_scope(f"sums{stage}"):
+                totals = finish_sums(number, stage - 1)
+            collect(vector, to_own)
+            return totals
+
         residual = source[own]
         image = first[own]
-        start_sums([over_own(residual * residual), over_own(residual * image)], 0)
-        apply(first, 1)
-        with jax.named_scope("sums0"):
-            norm_now, curvature = finish_sums(2, 0)
+        values = [over_own(residual * residual), over_own(residual * image)]
+        halo(first, 1, DISTANT)
+        start_sums(values, 0)
+        halo(first, 1, CLOSE)
+        norm_now, curvature = apply(first, 1, 2)
         step_size = norm_now / curvature
         direction, along = residual, image
         further = own_image[...]
@@ -405,11 +538,11 @@
         residual = residual - step_size * along
         image = image - step_size * further
         second[own] = image
-        halo(second, 2)
-        start_sums([over_own(residual * residual), over_own(residual * image)], 1)
-        apply(second, 2)
-        with jax.named_scope("sums1"):
-            norm_next, curvature = finish_sums(2, 1)
+        values = [over_own(residual * residual), over_own(residual * image)]
+        halo(second, 2, DISTANT)
+        start_sums(values, 1)
+        halo(second, 2, CLOSE)
+        norm_next, curvature = apply(second, 2, 2)
         growth = norm_next / norm_now
         step_size = norm_next / (curvature - growth * norm_next / step_size)
         norm_now = norm_next
@@ -469,6 +602,7 @@
         pltpu.SemaphoreType.DMA((ITERS, KINDS)),
         pltpu.SemaphoreType.DMA((ITERS, len(groups))),
         pltpu.SemaphoreType.DMA((ITERS, len(groups))),
+        pltpu.SemaphoreType.REGULAR((2,)),
     ]
     return kernel, scratch
 

time: 31.1 us -> 30.6 us (0.984)
  Pallas kernels: 30.3 us -> 29.8 us
    pallas_call x1, Pallas kernels: 29.7 us -> 29.2 us  [per_device(): pl.pallas_call(kernel, out_shape=(jax.ShapeDtypeStruct(cells + (atoms,),...]
where the time goes in v4:
time: 30.6 us; the launch traced here: 30.4 us
  Pallas kernels  29.8 us (97%)
  between operations  0.64 us (2%)
    pallas_call x1, Pallas kernels, per_device(): pl.pallas_call(kernel, out_shape=(jax.ShapeDtypeStruct(cells + (atoms,),...  29.2 us
    pallas_call x1, Pallas kernels, per_device(): pl.pallas_call(put_out, out_shape=tuple((jax.ShapeDtypeStruct(v.shape, v....  0.62 us

profile of v4, /device:TPU:0, one launch (start us, length us, event | category | flops | bytes accessed | tf_op | source)
XLA Modules:
  0.0 30.4 jit_solution(3138632510063482461)
XLA Ops:
  0.6 29.2 %shard_map.77 = (f32[1,2,2,128]{3,2,1,0:T(2,128)S(1)}, f32[2,1,2,2,128]{4,3,2,1,0:T(2,128)S(1)}) custom-call(f32[3,1,2,2,128]{4,3,2,1,0:T(2,128)} %refs_0_.1, s32[1,2,2,128]{3,2,1,0:T(2,128)} %refs_1_.1, s32[1,2,2,27]{3,2,1,0:T(2,128)} %refs_2_.1, f32[2]{0:T(128)} %refs_3_.1, f32[2]{0:T(128)} %refs_4_.1, f32[2]{0:T(128)} %refs_5_.1), custom_call_target="tpu_custom_call" | custom-call | tf_op jit(solution)/shard_map/pallas_call | solution.py:634
  29.8 0.6 %shard_map.78 = (f32[1,2,2,128]{3,2,1,0:T(2,128)}, f32[2,1,2,2,128]{4,3,2,1,0:T(2,128)}) custom-call(f32[1,2,2,128]{3,2,1,0:T(2,128)S(1)} %get-tuple-element.4.charge_in, f32[2,1,2,2,128]{4,3,2,1,0:T(2,128)S(1)} %get-tuple-element.5.resid_in), custom_call_target="tpu_custom_call" | custom-call | tf_op jit(solution)/shard_map/pallas_call | solution.py:647

commit v5 on v4

--- a/solution.py
+++ b/solution.py
@@ -16,24 +16,7 @@
 MESH = pl.DeviceIdType.MESH
 STEPS = [d for d in itertools.product((-1, 0, 1), repeat=3)]
 REMOTE = sorted((d for d in STEPS if d != (0, 0, 0)), key=lambda d: (-abs(d[2]), -abs(d[0])))
-DISTANT = [d for d in REMOTE if d[2]]
-CLOSE = [d for d in REMOTE if not d[2]]
 KINDS = 6
-
-
-def rounded_sides(step, cells):
-    source, target = [], []
-    for d, c in zip(step, cells):
-        if d == 0:
-            source.append(pl.ds(1, c))
-            target.append(pl.ds(1, c))
-        elif d > 0:
-            source.append(pl.ds(c, 1))
-            target.append(pl.ds(0, 1))
-        else:
-            source.append(pl.ds(1, 1))
-            target.append(pl.ds(c + 1, 1))
-    return tuple(source), tuple(target)
 
 
 def make_kernel(sizes, groups, cells, atoms, types, rows):
@@ -41,7 +24,33 @@
     tiles = cells[0] * cells[1] * cells[2]
     local = list(itertools.product(*[range(c) for c in cells]))
     padded = list(itertools.product(*[range(w) for w in width]))
-    own = tuple(slice(1, 1 + c) for c in cells)
+    own = (slice(1, 1 + cells[0]), slice(0, cells[1]), slice(1, 1 + cells[2]))
+    joined = sizes["gy"] == 2 and cells[1] == 2
+    steps = [d for d in REMOTE if not (joined and d[1] < 0)]
+    distant = [d for d in steps if d[2]]
+    close = [d for d in steps if not d[2]]
+
+    def slot(place):
+        return (place[0], (place[1] - 1) % width[1], place[2])
+
+    def rounded_sides(step):
+        source, target = [], []
+        for axis, (d, c) in enumerate(zip(step, cells)):
+            first, low, high = (0, c + 1, c) if axis == 1 else (1, 0, c + 1)
+            if d == 0:
+                source.append(pl.ds(first, c))
+                target.append(pl.ds(first, c))
+            elif axis == 1 and joined:
+                source.append(pl.ds(0, 2))
+                target.append(pl.ds(2, 2))
+            elif d > 0:
+                source.append(pl.ds(first + c - 1, 1))
+                target.append(pl.ds(low, 1))
+            else:
+                source.append(pl.ds(first, 1))
+                target.append(pl.ds(high, 1))
+        return tuple(source), tuple(target)
+
     group_sizes = []
     for axes in groups:
         count = 1
@@ -95,16 +104,19 @@
                 return (side if place[0] == 0 else 2 - side,) + place[1:]
             return place
 
+        upward = jnp.where(me["gz"] == sizes["gz"] - 1, 5, 2)
+        downward = jnp.where(me["gz"] == 1, 2, 5)
+        eastward = jnp.where(side == 2, 3, 4)
+        westward = jnp.where(side == 2, 4, 3)
+
         def arrival(step):
-            if step[2] > 0:
-                return jnp.where(me["gz"] == sizes["gz"] - 1, 5, 2)
-            if step[2] < 0:
-                return jnp.where(me["gz"] == 1, 2, 5)
+            if step[2]:
+                return upward if step[2] > 0 else downward
             if step[1]:
                 return 1 if step[0] else 0
             if not paired:
                 return 3 if step[0] > 0 else 4
-            return jnp.where(side - 1 == step[0], 3, 4)
+            return eastward if step[0] > 0 else westward
 
         def departure(step):
             if step[2]:
@@ -141,22 +153,18 @@
                 return [real(p) for p in padded if reach(p) == which]
             return [p + (far[which - 3],) for p in itertools.product(*map(range, width[:2]))]
 
+        turned = {
+            a: [lax.rem(me[a] + d, sizes[a]) if d else me[a] for d in range(sizes[a])] for a in AXES
+        }
+
         def neighbour(step):
-            return tuple(
-                lax.rem(me[a] + (d + sizes[a]), sizes[a]) for a, d in zip(AXES, step)
-            )
+            return tuple(turned[a][d % sizes[a]] for a, d in zip(AXES, step))
 
         def member(axes, hop):
-            rank = 0
-            count = 1
-            for a in axes:
-                rank = rank * sizes[a] + me[a]
-                count = count * sizes[a]
-            rank = lax.rem(rank + hop, count)
             place = dict(me)
             for a in reversed(axes):
-                place[a] = lax.rem(rank, sizes[a])
-                rank = rank // sizes[a]
+                place[a] = turned[a][hop % sizes[a]]
+                hop = hop // sizes[a]
             return tuple(place[a] for a in AXES)
 
         def lookup(kinds, table):
@@ -254,12 +262,12 @@
 
         for x, y, z in local:
             for f in range(3):
-                fields[x + 1, y + 1, z + 1, f : f + 1, :] = off_ref[f, x, y, z : z + 1, :]
-            fields[x + 1, y + 1, z + 1, 3:4, :] = type_ref[x, y, z : z + 1, :].astype(jnp.float32)
+                fields[x + 1, y, z + 1, f : f + 1, :] = off_ref[f, x, y, z : z + 1, :]
+            fields[x + 1, y, z + 1, 3:4, :] = type_ref[x, y, z : z + 1, :].astype(jnp.float32)
 
         def locate(places):
             for place in places:
-                x, y, z = place
+                x, y, z = slot(place)
                 kinds = fields[x, y, z, 3:4, :]
                 v1, v2, v3 = thirds(stacked(fields[x, y, z], place))
                 unit = jnp.where(row4 < 3, 1.0, 0.0)
@@ -276,9 +284,9 @@
             else:
                 pl.semaphore_wait(barrier, greeted)
 
-        def halo(buffer, stage, steps=REMOTE):
-            for step in steps:
-                here, there = rounded_sides(step, cells)
+        def halo(buffer, stage, chosen):
+            for step in chosen:
+                here, there = rounded_sides(step)
                 pltpu.make_async_remote_copy(
                     src_ref=buffer.at[here],
                     dst_ref=buffer.at[there],
@@ -303,9 +311,10 @@
                 whole_kind(buffer, stage, kind).wait_recv()
 
         def coupling(t, n, place, at, own_part, itself):
+            x, y, z = place
             square = lax.dot_general(
                 own_part[0][:, :32],
-                geometry[place],
+                geometry[x, y, z],
                 (((1,), (0,)), ((), ())),
                 preferred_element_type=jnp.float32,
             )
@@ -318,7 +327,7 @@
             w = w * w
             w = w * w
             shape = (u + 0.5) * (square + 0.2) - 0.05
-            cube = square * u + own_part[1] * shields[place[0], place[1], place[2], 0:1, :]
+            cube = square * u + own_part[1] * shields[x, y, z, 0:1, :]
             return w * shape * jnp.exp2(jnp.log2(cube) * (-1.0 / 3.0))
 
         lanes = lax.broadcasted_iota(jnp.int32, (rows, atoms), 1)
@@ -345,7 +354,8 @@
                         total_t = sums[t, 1, pl.ds(at, rows), :]
                     if building:
                         own_part = [columns[t, f, pl.ds(at, rows), :] for f in range(2)]
-                    for n, (x, y, z), itself in part:
+                    for n, place, itself in part:
+                        x, y, z = slot(place)
                         if building:
                             block = coupling(t, n, (x, y, z), at, own_part, itself)
                             blocks[t, n, pl.ds(at, rows), :] = block
@@ -390,12 +400,12 @@
                 preferred_element_type=jnp.float32,
             )
             for t, (x, y, z) in enumerate(local):
-                here = vector[x + 1, y + 1, z + 1]
+                here = vector[x + 1, y, z + 1]
                 image(x, y, z, eta[t] * here + scale * result[2 * t : 2 * t + 2])
 
         def to_padded(buffer):
             def store(x, y, z, pair):
-                buffer[x + 1, y + 1, z + 1] = pair
+                buffer[x + 1, y, z + 1] = pair
 
             return store
 
@@ -455,20 +465,20 @@
 
         def distant_positions():
             others_are_in()
-            halo(fields, 0, DISTANT)
+            halo(fields, 0, distant)
 
         last = me["gz"] == sizes["gz"] - 1
         if planes:
-            halo(fields, 0, CLOSE)
+            halo(fields, 0, close)
             pl.when(last)(distant_positions)
         else:
-            halo(fields, 0)
+            halo(fields, 0, steps)
         for load in loads[2:]:
             load.wait()
         locate(places_of(0))
         for t, (x, y, z) in enumerate(local):
             place = (x + 1, y + 1, z + 1)
-            v1, v2, v3 = thirds(stacked(fields[place], place))
+            v1, v2, v3 = thirds(stacked(fields[slot(place)], place))
             c1 = jnp.where(row4 < 3, -2.0 * v1, 1.0)
             c2 = jnp.where(row4 < 3, -2.0 * v2, 0.0)
             c3 = jnp.where(row4 < 3, -2.0 * v3, 0.0)
@@ -479,7 +489,7 @@
             columns[t, 0] = jnp.transpose(
                 jnp.concatenate([c1, c1, c1, c2, c2, c3, norms, none], axis=0)
             )
-            row = shields[x + 1, y + 1, z + 1, 0:1, :]
+            row = shields[x + 1, y, z + 1, 0:1, :]
             columns[t, 1] = jnp.transpose(jnp.broadcast_to(row, (atoms, atoms)))
         entries = jnp.concatenate(
             [list_ref[x, y, z : z + 1, :] - linear((x + 1, y + 1, z + 1)) for x, y, z in local], 0
@@ -489,7 +499,7 @@
                 jnp.where(entries == linear(step), 1.0, 0.0), axis=1, keepdims=True
             )
             listed[n] = jnp.broadcast_to(1.0 - (1.0 - found) * FAR, (tiles, atoms))
-        eta = [lookup(fields[x + 1, y + 1, z + 1, 3:4, :], eta_ref) for x, y, z in local]
+        eta = [lookup(fields[x + 1, y, z + 1, 3:4, :], eta_ref) for x, y, z in local]
 
         with jax.named_scope("build0"):
             tile_pass(source, (0,), True)
@@ -519,17 +529,17 @@
                     arrived(vector, stage, which)
                 with jax.named_scope(f"pass{stage}_{which}"):
                     tile_pass(vector, (which,), False)
+            with jax.named_scope(f"collect{stage}"):
+                collect(vector, to_own)
             with jax.named_scope(f"sums{stage}"):
-                totals = finish_sums(number, stage - 1)
-            collect(vector, to_own)
-            return totals
+                return finish_sums(number, stage - 1)
 
         residual = source[own]
         image = first[own]
         values = [over_own(residual * residual), over_own(residual * image)]
-        halo(first, 1, DISTANT)
+        halo(first, 1, distant)
         start_sums(values, 0)
-        halo(first, 1, CLOSE)
+        halo(first, 1, close)
         norm_now, curvature = apply(first, 1, 2)
         step_size = norm_now / curvature
         direction, along = residual, image
@@ -539,9 +549,9 @@
         image = image - step_size * further
         second[own] = image
         values = [over_own(residual * residual), over_own(residual * image)]
-        halo(second, 2, DISTANT)
+        halo(second, 2, distant)
         start_sums(values, 1)
-        halo(second, 2, CLOSE)
+        halo(second, 2, close)
         norm_next, curvature = apply(second, 2, 2)
         growth = norm_next / norm_now
         step_size = norm_next / (curvature - growth * norm_next / step_size)

time: 30.6 us -> 30.2 us (0.987)
  Pallas kernels: 29.8 us -> 29.4 us
    pallas_call x1, Pallas kernels: 29.2 us -> 28.7 us  [per_device(): pl.pallas_call(kernel, out_shape=(jax.ShapeDtypeStruct(cells + (atoms,),...]
where the time goes in v5:
time: 30.2 us; the launch traced here: 30 us
  Pallas kernels  29.4 us (97%)
  between operations  0.64 us (2%)
    pallas_call x1, Pallas kernels, per_device(): pl.pallas_call(kernel, out_shape=(jax.ShapeDtypeStruct(cells + (atoms,),...  28.7 us
    pallas_call x1, Pallas kernels, per_device(): pl.pallas_call(put_out, out_shape=tuple((jax.ShapeDtypeStruct(v.shape, v....  0.62 us

profile of v5, /device:TPU:0, one launch (start us, length us, event | category | flops | bytes accessed | tf_op | source)
XLA Modules:
  0.0 30.0 jit_solution(15440028177628669791)
XLA Ops:
  0.6 28.7 %shard_map.77 = (f32[1,2,2,128]{3,2,1,0:T(2,128)S(1)}, f32[2,1,2,2,128]{4,3,2,1,0:T(2,128)S(1)}) custom-call(f32[3,1,2,2,128]{4,3,2,1,0:T(2,128)} %refs_0_.1, s32[1,2,2,128]{3,2,1,0:T(2,128)} %refs_1_.1, s32[1,2,2,27]{3,2,1,0:T(2,128)} %refs_2_.1, f32[2]{0:T(128)} %refs_3_.1, f32[2]{0:T(128)} %refs_4_.1, f32[2]{0:T(128)} %refs_5_.1), custom_call_target="tpu_custom_call" | custom-call | tf_op jit(solution)/shard_map/pallas_call | solution.py:644
  29.4 0.6 %shard_map.78 = (f32[1,2,2,128]{3,2,1,0:T(2,128)}, f32[2,1,2,2,128]{4,3,2,1,0:T(2,128)}) custom-call(f32[1,2,2,128]{3,2,1,0:T(2,128)S(1)} %get-tuple-element.4.charge_in, f32[2,1,2,2,128]{4,3,2,1,0:T(2,128)S(1)} %get-tuple-element.5.resid_in), custom_call_target="tpu_custom_call" | custom-call | tf_op jit(solution)/shard_map/pallas_call | solution.py:657

commit v6 on v5

--- a/solution.py
+++ b/solution.py
@@ -16,7 +16,6 @@
 MESH = pl.DeviceIdType.MESH
 STEPS = [d for d in itertools.product((-1, 0, 1), repeat=3)]
 REMOTE = sorted((d for d in STEPS if d != (0, 0, 0)), key=lambda d: (-abs(d[2]), -abs(d[0])))
-KINDS = 6
 
 
 def make_kernel(sizes, groups, cells, atoms, types, rows):
@@ -57,17 +56,16 @@
         for a in axes:
             count = count * sizes[a]
         group_sizes.append(count)
-    boxes = (
-        (pl.ds(0, cells[0]), pl.ds(0, 2), pl.ds(0, cells[2])),
-        (pl.ds(0, 2), pl.ds(0, 2), pl.ds(0, cells[2])),
-        (pl.ds(0, width[0]), pl.ds(0, width[1]), pl.ds(0, 1)),
-        (pl.ds(0, 1), pl.ds(0, cells[1]), pl.ds(0, cells[2])),
-        (pl.ds(0, 1), pl.ds(0, cells[1]), pl.ds(0, cells[2])),
-        (pl.ds(0, width[0]), pl.ds(0, width[1]), pl.ds(0, 1)),
-    )
     paired = cells[0] == 1 and sizes["gx"] % 2 == 0
     planes = paired and len(groups) == 1
     base = atoms // (2 * tiles)
+    partner_tiles = cells[1] * cells[2] if paired else 0
+    plane_tiles = width[0] * width[1] * cells[2] - tiles
+    side_tiles = width[0] * width[1]
+    brought = [partner_tiles, plane_tiles - partner_tiles, side_tiles, side_tiles]
+    brought += [plane_tiles, side_tiles, side_tiles] * (ITERS - 1)
+    depth = [4] + [2] * (ITERS - 1)
+    sent = sum(depth) * (plane_tiles + 2 * side_tiles) + ITERS * sum(n - 1 for n in group_sizes)
 
     def linear(place):
         return (place[0] * width[1] + place[1]) * width[2] + place[2]
@@ -88,7 +86,7 @@
         (fields, geometry, shields, columns, listed, blocks, sums, source) = refs[14:22]
         (first, second, own_image) = refs[22:25]
         parts = refs[25 : 25 + len(groups)]
-        load_sem, halo_send, halo_recv, sum_send, sum_recv, met = refs[25 + len(groups) :]
+        load_sem, send_sem, halo_recv, sum_recv, met, gauge = refs[25 + len(groups) :]
 
         loads = [
             pltpu.make_async_copy(a, b, load_sem.at[k])
@@ -104,26 +102,18 @@
                 return (side if place[0] == 0 else 2 - side,) + place[1:]
             return place
 
-        upward = jnp.where(me["gz"] == sizes["gz"] - 1, 5, 2)
-        downward = jnp.where(me["gz"] == 1, 2, 5)
-        eastward = jnp.where(side == 2, 3, 4)
-        westward = jnp.where(side == 2, 4, 3)
-
-        def arrival(step):
+        upward = jnp.where(me["gz"] == sizes["gz"] - 1, 1, 0)
+        downward = jnp.where(me["gz"] == 1, 0, 1)
+        eastward = jnp.where(side == 2, 0, 1)
+        westward = jnp.where(side == 2, 1, 0)
+
+        def arrival(step, stage):
+            start = 4 + 3 * (stage - 1) if stage else 1
             if step[2]:
-                return upward if step[2] > 0 else downward
-            if step[1]:
-                return 1 if step[0] else 0
-            if not paired:
-                return 3 if step[0] > 0 else 4
+                return start + 1 + (upward if step[2] > 0 else downward)
+            if stage or not paired or step[1]:
+                return start
             return eastward if step[0] > 0 else westward
-
-        def departure(step):
-            if step[2]:
-                return 2 if step[2] > 0 else 5
-            if step[1]:
-                return 1 if step[0] else 0
-            return 3 if step[0] > 0 else 4
 
         pairs = [[] for _ in range(5)]
         for t, home in enumerate(local):
@@ -290,25 +280,27 @@
                 pltpu.make_async_remote_copy(
                     src_ref=buffer.at[here],
                     dst_ref=buffer.at[there],
-                    send_sem=halo_send.at[stage, departure(step)],
-                    recv_sem=halo_recv.at[stage, arrival(step)],
+                    send_sem=send_sem.at[0],
+                    recv_sem=halo_recv.at[arrival(step, stage)],
                     device_id=neighbour(step),
                     device_id_type=MESH,
                 ).start()
 
-        def whole_kind(buffer, stage, kind):
+        def all_of(count, semaphores):
             return pltpu.make_async_remote_copy(
-                src_ref=buffer.at[boxes[kind]],
-                dst_ref=buffer.at[boxes[kind]],
-                send_sem=halo_send.at[stage, kind],
-                recv_sem=halo_recv.at[stage, kind],
+                src_ref=gauge.at[pl.ds(0, count)],
+                dst_ref=gauge.at[pl.ds(0, count)],
+                send_sem=semaphores[0],
+                recv_sem=semaphores[1],
                 device_id=neighbour(REMOTE[0]),
                 device_id_type=MESH,
             )
 
-        def arrived(buffer, stage, which):
-            for kind in ((), (3,), (0, 1, 4) if paired else (0, 1, 3, 4), (2,), (5,))[which]:
-                whole_kind(buffer, stage, kind).wait_recv()
+        def arrived(stage, which):
+            index = (4 + 3 * (stage - 1) - 1 if stage else 0) + which
+            all_of(
+                brought[index] * depth[stage], (send_sem.at[0], halo_recv.at[index])
+            ).wait_recv()
 
         def coupling(t, n, place, at, own_part, itself):
             x, y, z = place
@@ -412,7 +404,8 @@
         def to_own(x, y, z, pair):
             own_image[x, y, z] = pair
 
-        lane = lax.broadcasted_iota(jnp.int32, (2, atoms), 1)
+        lane = lax.broadcasted_iota(jnp.int32, (1, atoms), 1)
+        half = atoms // 2
 
         def over_own(values):
             return jnp.sum(jnp.sum(values, axis=(0, 1, 2)), axis=1, keepdims=True)
@@ -423,7 +416,7 @@
                 pltpu.make_async_remote_copy(
                     src_ref=parts[g].at[stage, 0],
                     dst_ref=parts[g].at[stage, hop],
-                    send_sem=sum_send.at[stage, g],
+                    send_sem=send_sem.at[0],
                     recv_sem=sum_recv.at[stage, g],
                     device_id=member(axes, hop),
                     device_id_type=MESH,
@@ -431,37 +424,28 @@
                 for hop in range(1, count)
             ]
 
-        def whole_sum(g, stage):
-            count = group_sizes[g]
-            return pltpu.make_async_remote_copy(
-                src_ref=parts[g].at[stage, pl.ds(1, count - 1)],
-                dst_ref=parts[g].at[stage, pl.ds(1, count - 1)],
-                send_sem=sum_send.at[stage, g],
-                recv_sem=sum_recv.at[stage, g],
-                device_id=member(groups[g], 1),
-                device_id_type=MESH,
-            )
-
         def start_sums(values, stage):
-            message = jnp.zeros((2, atoms), jnp.float32)
+            message = jnp.zeros((1, atoms), jnp.float32)
             for k, value in enumerate(values):
-                message = jnp.where(lane == k, value, message)
+                for row in range(2):
+                    message = jnp.where(lane == k + row * half, value[row : row + 1], message)
             parts[0][stage, 0] = message
             for copy in sum_copies(0, stage):
                 copy.start()
 
         def finish_sums(number, stage):
             for g in range(len(groups)):
-                whole_sum(g, stage).wait_recv()
+                all_of(group_sizes[g] - 1, (send_sem.at[0], sum_recv.at[stage, g])).wait_recv()
                 total = jnp.sum(parts[g][stage], axis=0)
                 if g + 1 < len(groups):
                     parts[g + 1][stage, 0] = total
                     for copy in sum_copies(g + 1, stage):
                         copy.start()
-            return [
-                jnp.sum(jnp.where(lane == k, total, 0.0), axis=1, keepdims=True)
-                for k in range(number)
-            ]
+            def picked(k):
+                return jnp.sum(jnp.where(lane == k, total, 0.0), axis=1, keepdims=True)
+
+            first_row = lax.broadcasted_iota(jnp.int32, (2, 1), 0) == 0
+            return [jnp.where(first_row, picked(k), picked(k + half)) for k in range(number)]
 
         def distant_positions():
             others_are_in()
@@ -508,7 +492,7 @@
                 with jax.named_scope("others"):
                     pl.when(jnp.logical_not(last))(distant_positions)
             with jax.named_scope(f"wait_pos{which}"):
-                arrived(fields, 0, which)
+                arrived(0, which - 1)
             locate(places_of(which))
             with jax.named_scope(f"build{which}"):
                 tile_pass(source, (which,), True)
@@ -519,14 +503,12 @@
             with jax.named_scope(f"pass{stage}_0"):
                 tile_pass(vector, (0,), False)
             with jax.named_scope(f"wait{stage}_1"):
-                if paired:
-                    arrived(vector, stage, 1)
-                arrived(vector, stage, 2)
+                arrived(stage, 1)
             with jax.named_scope(f"pass{stage}_1"):
                 tile_pass(vector, (1, 2) if paired else (2,), False)
             for which in (3, 4):
                 with jax.named_scope(f"wait{stage}_{which}"):
-                    arrived(vector, stage, which)
+                    arrived(stage, which - 1)
                 with jax.named_scope(f"pass{stage}_{which}"):
                     tile_pass(vector, (which,), False)
             with jax.named_scope(f"collect{stage}"):
@@ -542,6 +524,7 @@
         halo(first, 1, close)
         norm_now, curvature = apply(first, 1, 2)
         step_size = norm_now / curvature
+        closing = 1.0 / (norm_now * step_size)
         direction, along = residual, image
         further = own_image[...]
         answer = step_size * direction
@@ -554,7 +537,8 @@
         halo(second, 2, close)
         norm_next, curvature = apply(second, 2, 2)
         growth = norm_next / norm_now
-        step_size = norm_next / (curvature - growth * norm_next / step_size)
+        step_size = norm_next / (curvature - norm_next * norm_next * closing)
+        closing = 1.0 / (norm_next * step_size)
         norm_now = norm_next
         further = own_image[...] + growth * further
         direction = residual + growth * direction
@@ -567,7 +551,7 @@
         with jax.named_scope("sums2"):
             norm_next, curvature, *others = finish_sums(5, 2)
         growth = norm_next / norm_now
-        step_size = norm_next / (curvature - growth * norm_next / step_size)
+        step_size = norm_next / (curvature - norm_next * norm_next * closing)
         answer = answer + step_size * (residual + growth * direction)
         residual = residual - step_size * (image + growth * along)
         totals = others[0] + step_size * (others[1] + growth * others[2])
@@ -579,12 +563,7 @@
             for s in range(2):
                 resid_ref[s, x, y, z : z + 1, :] = residual[x, y, z, s : s + 1]
         with jax.named_scope("drain"):
-            for stage, buffer in enumerate((fields, first, second)):
-                for kind in range(KINDS):
-                    whole_kind(buffer, stage, kind).wait_send()
-            for stage in range(ITERS):
-                for g in range(len(groups)):
-                    whole_sum(g, stage).wait_send()
+            all_of(sent, (send_sem.at[0], halo_recv.at[0])).wait_send()
 
     scratch = [
         pltpu.VMEM((3,) + cells + (atoms,), jnp.float32),
@@ -605,14 +584,14 @@
         pltpu.VMEM(width + (2, atoms), jnp.float32),
         pltpu.VMEM(cells + (2, atoms), jnp.float32),
     ]
-    scratch += [pltpu.VMEM((ITERS, count, 2, atoms), jnp.float32) for count in group_sizes]
+    scratch += [pltpu.VMEM((ITERS, count, 1, atoms), jnp.float32) for count in group_sizes]
     scratch += [
         pltpu.SemaphoreType.DMA((6,)),
-        pltpu.SemaphoreType.DMA((ITERS, KINDS)),
-        pltpu.SemaphoreType.DMA((ITERS, KINDS)),
-        pltpu.SemaphoreType.DMA((ITERS, len(groups))),
+        pltpu.SemaphoreType.DMA((1,)),
+        pltpu.SemaphoreType.DMA((len(brought),)),
         pltpu.SemaphoreType.DMA((ITERS, len(groups))),
         pltpu.SemaphoreType.REGULAR((2,)),
+        pltpu.VMEM((sent, 1, atoms), jnp.float32),
     ]
     return kernel, scratch
 

time: 30.2 us -> 29.8 us (0.987)
  Pallas kernels: 29.4 us -> 28.9 us
    pallas_call x1, Pallas kernels: 28.7 us -> 28.3 us  [per_device(): pl.pallas_call(kernel, out_shape=(jax.ShapeDtypeStruct(cells + (atoms,),...]
where the time goes in v6:
time: 29.8 us; the launch traced here: 29.6 us
  Pallas kernels  28.9 us (97%)
  between operations  0.64 us (2%)
    pallas_call x1, Pallas kernels, per_device(): pl.pallas_call(kernel, out_shape=(jax.ShapeDtypeStruct(cells + (atoms,),...  28.3 us
    pallas_call x1, Pallas kernels, per_device(): pl.pallas_call(put_out, out_shape=tuple((jax.ShapeDtypeStruct(v.shape, v....  0.62 us

profile of v6, /device:TPU:0, one launch (start us, length us, event | category | flops | bytes accessed | tf_op | source)
XLA Modules:
  0.0 29.6 jit_solution(2937881358739651958)
XLA Ops:
  0.6 28.3 %shard_map.77 = (f32[1,2,2,128]{3,2,1,0:T(2,128)S(1)}, f32[2,1,2,2,128]{4,3,2,1,0:T(2,128)S(1)}) custom-call(f32[3,1,2,2,128]{4,3,2,1,0:T(2,128)} %refs_0_.1, s32[1,2,2,128]{3,2,1,0:T(2,128)} %refs_1_.1, s32[1,2,2,27]{3,2,1,0:T(2,128)} %refs_2_.1, f32[2]{0:T(128)} %refs_3_.1, f32[2]{0:T(128)} %refs_4_.1, f32[2]{0:T(128)} %refs_5_.1), custom_call_target="tpu_custom_call" | custom-call | tf_op jit(solution)/shard_map/pallas_call | solution.py:623
  28.9 0.6 %shard_map.78 = (f32[1,2,2,128]{3,2,1,0:T(2,128)}, f32[2,1,2,2,128]{4,3,2,1,0:T(2,128)}) custom-call(f32[1,2,2,128]{3,2,1,0:T(2,128)S(1)} %get-tuple-element.4.charge_in, f32[2,1,2,2,128]{4,3,2,1,0:T(2,128)S(1)} %get-tuple-element.5.resid_in), custom_call_target="tpu_custom_call" | custom-call | tf_op jit(solution)/shard_map/pallas_call | solution.py:636

commit v7 on v6

--- a/solution.py
+++ b/solution.py
@@ -221,6 +221,12 @@
 
         for load in loads[2:]:
             load.start()
+        with jax.named_scope("barrier"):
+            if planes:
+                plane_is_in()
+            else:
+                pl.semaphore_wait(barrier, greeted)
+
         for load in loads[:2]:
             load.wait()
 
@@ -268,12 +274,6 @@
                 source[x, y, z, 0:1, :] = -lookup(kinds, chi_ref)
                 source[x, y, z, 1:2, :] = jnp.full((1, atoms), -1.0, jnp.float32)
 
-        with jax.named_scope("barrier"):
-            if planes:
-                plane_is_in()
-            else:
-                pl.semaphore_wait(barrier, greeted)
-
         def halo(buffer, stage, chosen):
             for step in chosen:
                 here, there = rounded_sides(step)
@@ -314,6 +314,7 @@
                 i = lax.broadcasted_iota(jnp.int32, (rows, atoms), 0) + at
                 j = lax.broadcasted_iota(jnp.int32, (rows, atoms), 1)
                 square = jnp.where(i == j, 4.0, square)
+            square = jnp.maximum(square, 1e-6)
             u = square * lax.rsqrt(square)
             w = jnp.maximum(listed[n, pl.ds(t, 1), :] - u, 0.0)
             w = w * w
@@ -520,8 +521,8 @@
         image = first[own]
         values = [over_own(residual * residual), over_own(residual * image)]
         halo(first, 1, distant)
+        halo(first, 1, close)
         start_sums(values, 0)
-        halo(first, 1, close)
         norm_now, curvature = apply(first, 1, 2)
         step_size = norm_now / curvature
         closing = 1.0 / (norm_now * step_size)
@@ -533,8 +534,8 @@
         second[own] = image
         values = [over_own(residual * residual), over_own(residual * image)]
         halo(second, 2, distant)
+        halo(second, 2, close)
         start_sums(values, 1)
-        halo(second, 2, close)
         norm_next, curvature = apply(second, 2, 2)
         growth = norm_next / norm_now
         step_size = norm_next / (curvature - norm_next * norm_next * closing)

time: 29.8 us -> 29.9 us (level)
  no operation moved by 1% of the time
where the time goes in v7:
time: 29.9 us; the launch traced here: 29.7 us
  Pallas kernels  29.1 us (97%)
  between operations  0.64 us (2%)
    pallas_call x1, Pallas kernels, per_device(): pl.pallas_call(kernel, out_shape=(jax.ShapeDtypeStruct(cells + (atoms,),...  28.5 us
    pallas_call x1, Pallas kernels, per_device(): pl.pallas_call(put_out, out_shape=tuple((jax.ShapeDtypeStruct(v.shape, v....  0.62 us

profile of v7, /device:TPU:0, one launch (start us, length us, event | category | flops | bytes accessed | tf_op | source)
XLA Modules:
  0.0 29.7 jit_solution(17152910884788523642)
XLA Ops:
  0.6 28.5 %shard_map.77 = (f32[1,2,2,128]{3,2,1,0:T(2,128)S(1)}, f32[2,1,2,2,128]{4,3,2,1,0:T(2,128)S(1)}) custom-call(f32[3,1,2,2,128]{4,3,2,1,0:T(2,128)} %refs_0_.1, s32[1,2,2,128]{3,2,1,0:T(2,128)} %refs_1_.1, s32[1,2,2,27]{3,2,1,0:T(2,128)} %refs_2_.1, f32[2]{0:T(128)} %refs_3_.1, f32[2]{0:T(128)} %refs_4_.1, f32[2]{0:T(128)} %refs_5_.1), custom_call_target="tpu_custom_call" | custom-call | tf_op jit(solution)/shard_map/pallas_call | solution.py:624
  29.1 0.6 %shard_map.78 = (f32[1,2,2,128]{3,2,1,0:T(2,128)}, f32[2,1,2,2,128]{4,3,2,1,0:T(2,128)}) custom-call(f32[1,2,2,128]{3,2,1,0:T(2,128)S(1)} %get-tuple-element.4.charge_in, f32[2,1,2,2,128]{4,3,2,1,0:T(2,128)S(1)} %get-tuple-element.5.resid_in), custom_call_target="tpu_custom_call" | custom-call | tf_op jit(solution)/shard_map/pallas_call | solution.py:637
